TPU v7x, 256 devices: a whole 4x4x8 slice. The times are simulated.
256 devices in a mesh: pb: 32 (over z_hi, y, x), row: 8 (over z_lo, core).
Axes of the slice: x: 4, y: 4, z: 8 (z_hi: 2, z_lo: 4; z = z_hi * 4 + z_lo), core: 2. Of those that a mesh axis runs over, the one named last changes fastest.
Arguments:
- screened: bfloat16 [64, 2, 1024, 1024], P('pb', None, 'row'), may hold values from -1.0546875 to 1.0546875
- response: bfloat16 [64, 2, 1024, 1024], P(None, None, 'pb', 'row'), may hold values from -0.1875 to 0.1875
- q_owner: int32 [64], replicated, may hold values from 0 to 63, each once
- g_index: int32 [64, 1024], P('pb'), may hold values from 0 to 1023, each once within a row
Outputs:
- tangent: float32 [64, 2, 1024, 1024], P(None, None, ('row', 'pb'))
Inputs may be any that keep to these rules, and one draw needn't show every extreme that they name: `q_owner`: each owner slot appears once. `g_index`: each row is a permutation of the 1024 plane waves.
All inputs are finite; a program needn't handle non-finite values.
Results may differ from a plain program's by a relative error of at most 0.0029.
Values may be sent and summed in bfloat16 or wider, within the bound.
No kernel may reach another device: no remote copies, remote signals or barrier semaphores. Data moves between devices by JAX's collectives and lax.ppermute only.
A program may use at most 64 MiB of HBM per device.

v0:
```python
import jax
import jax.numpy as jnp
from jax import lax
from jax.experimental import pallas as pl
from jax.experimental.pallas import tpu as pltpu
from jax.sharding import Mesh, PartitionSpec as P


OWNER = ("zh", "y", "x")
ROW = ("zm", "zn", "c")
SPREAD = ("zh", "y", "x", "zm")

FAR = pl.BlockSpec(memory_space=pltpu.MemorySpace.HBM)
DENSE = pl.BlockSpec(memory_space=pltpu.VMEM)
VMEM = pltpu.VMEM
PARAMS = pltpu.CompilerParams(vmem_limit_bytes=32 * 2**20)


def swap(x, axes, mask):
    count = 2 ** len(axes)
    return lax.ppermute(x, axes, [(i, i ^ mask) for i in range(count)])


def near(xs):
    return [pltpu.with_memory_space_constraint(x, pltpu.VMEM) for x in xs]


def far(xs):
    return [pltpu.with_memory_space_constraint(x, pltpu.MemorySpace.HBM) for x in xs]


def spread(x):
    return lax.all_to_all(x, SPREAD, 0, 0, tiled=True)


def order_kernel(side_ref, table_ref, out_ref):
    size = out_ref.shape[0]
    step = 128
    for i in range(0, size, step):
        ids = lax.broadcasted_iota(jnp.int32, (step, size), 1)
        hit = ids == table_ref[i : i + step, :]
        out_ref[i : i + step, :] = jnp.where(hit, 1.0, 0.0).astype(jnp.bfloat16)


def order_matrix(side, table):
    size = table.shape[0]
    return pl.pallas_call(
        order_kernel,
        out_shape=VMEM((size, size), jnp.bfloat16),
        in_specs=[pl.BlockSpec(memory_space=pltpu.SMEM), DENSE],
        out_specs=DENSE,
        compiler_params=PARAMS,
        name="order",
    )(side, table)


def half_kernel(side_ref, order_ref, landed_ref, *refs):
    w_refs, outs = refs[:8], refs[8:12]
    w, chi, w_sems, chi_sems = refs[12:]
    width = landed_ref.shape[-1]
    side = side_ref[0]
    chi_copies, w_copies = [], []
    for b in range(2):
        for part in range(2):
            at = part * 2 + b
            chi_copies.append(
                pltpu.make_async_copy(
                    landed_ref.at[:, side ^ b, part],
                    chi.at[:, :, pl.ds(at * width, width)],
                    chi_sems.at[at],
                )
            )
    for k in range(8):
        w_copies.append(pltpu.make_async_copy(w_refs[k], w.at[k], w_sems.at[k]))
    for copy in chi_copies + w_copies:
        copy.start()
    size = order_ref.shape[0]
    for copy in chi_copies:
        copy.wait()
    both = chi[...].reshape(size, 4 * width)
    both = jnp.dot(order_ref[...], both, preferred_element_type=jnp.float32)
    real, imag = both[:, : 2 * width], both[:, 2 * width :]
    first = both.astype(jnp.bfloat16)
    second = jnp.concatenate([-imag, real], axis=1).astype(jnp.bfloat16)
    for k in range(8):
        w_copies[k].wait()
        half = jnp.dot(w[k, 0], first, preferred_element_type=jnp.float32)
        half += jnp.dot(w[k, 1], second, preferred_element_type=jnp.float32)
        half = half.astype(jnp.bfloat16)
        dm, delta = k % 2, k // 2
        outs[delta][0, dm] = half[:, : 2 * width]
        outs[delta][1, dm] = half[:, 2 * width :]


def half_product(side, order, blocks, landed):
    rows, size = blocks[0].shape[1:]
    owners, _, _, short, width = landed.shape
    return pl.pallas_call(
        half_kernel,
        out_shape=[VMEM((2, 2, rows, 2 * width), jnp.bfloat16)] * 4,
        in_specs=[pl.BlockSpec(memory_space=pltpu.SMEM), DENSE] + [FAR] * 9,
        out_specs=[DENSE] * 4,
        scratch_shapes=[
            pltpu.VMEM((8, 2, rows, size), jnp.bfloat16),
            pltpu.VMEM((owners, short, 4 * width), jnp.bfloat16),
            pltpu.SemaphoreType.DMA((8,)),
            pltpu.SemaphoreType.DMA((4,)),
        ],
        compiler_params=PARAMS,
        cost_estimate=pl.CostEstimate(
            flops=2 * size * size * 4 * width * 3, bytes_accessed=6 * 2**20, transcendentals=0
        ),
        name="half",
    )(side, *near([order]), *far([landed, *blocks]))


def tangent_kernel(side_ref, *refs):
    w_refs, h_refs, out_ref = refs[:8], refs[8:12], refs[12]
    w, mixed, w_sems = refs[13:]
    rows, size = w.shape[2:]
    copies = []
    for k in range(8):
        for part in range(2):
            copies.append(
                pltpu.make_async_copy(
                    w_refs[k].at[part], w.at[part, k], w_sems.at[2 * k + part]
                )
            )
    for copy in copies:
        copy.start()
    left = jnp.concatenate([h[...].reshape(4 * rows, 2 * rows) for h in h_refs], axis=1)
    for copy in copies:
        copy.wait()
    side = side_ref[0]
    wide = size // 2
    owners = out_ref.shape[0]
    for h in range(2):
        lanes = slice(h * wide, h * wide + wide)

        def by(part):
            right = w[part, :, :, lanes].reshape(size, wide)
            return jnp.dot(left, right, preferred_element_type=jnp.float32)

        by_real, by_imag = by(0), by(1)
        cut = 2 * rows
        real = by_real[:cut] - by_imag[cut:]
        imag = by_imag[:cut] + by_real[cut:]
        for j in range(2 * owners):
            mixed[j, 0:4, :] = real[4 * j : 4 * j + 4, :]
            mixed[j, 4:8, :] = imag[4 * j : 4 * j + 4, :]
        for b in range(2):
            piece = mixed[b * owners : (b + 1) * owners].astype(jnp.bfloat16)
            out_ref[:, side ^ b, :, lanes] = piece


def tangent_product(side, blocks, halves):
    rows, size = blocks[0].shape[1:]
    owners = rows // 4
    return pl.pallas_call(
        tangent_kernel,
        out_shape=VMEM((owners, 2, 8, size), jnp.bfloat16),
        in_specs=[pl.BlockSpec(memory_space=pltpu.SMEM)] + [FAR] * 8 + [DENSE] * 4,
        out_specs=DENSE,
        scratch_shapes=[
            pltpu.VMEM((2, 8, rows, size), jnp.bfloat16),
            pltpu.VMEM((2 * owners, 8, size // 2), jnp.float32),
            pltpu.SemaphoreType.DMA((16,)),
        ],
        compiler_params=PARAMS,
        cost_estimate=pl.CostEstimate(
            flops=2 * 4 * rows * size * size * 2, bytes_accessed=6 * 2**20, transcendentals=0
        ),
        name="tangent",
    )(side, *far(blocks), *near(halves))


def steps(screened, response, q_owner, g_index):
    slots = q_owner.shape[0]
    _, parts, _, size = screened.shape
    short, width = response.shape[2:]
    zm = lax.axis_index("zm")
    side = zm[None].astype(jnp.int32)

    def pick(x, k):
        return lax.dynamic_index_in_dim(x, k, 0, keepdims=False)

    mine = pick(screened, zm)
    other = swap(pick(screened, 1 - zm), ("zm",), 1)
    across = [swap(mine, ("zn",), 1)]
    order = order_matrix(side, pick(g_index, zm)[:, None])

    ids = jnp.arange(slots, dtype=jnp.int32)
    inverse = jnp.sum(jnp.where(q_owner[None, :] == ids[:, None], ids[None, :], 0), axis=1)
    ordered = response.at[inverse].get(mode="promise_in_bounds")
    landed = spread(ordered)
    landed = landed.reshape(slots // 2, 2, parts, short, width)

    across.append(swap(other, ("zn",), 1))
    blocks = [mine, other] + across
    blocks += [swap(block, ("c",), 1) for block in blocks]

    halves = half_product(side, order, blocks, landed)
    halves = [
        halves[0],
        swap(halves[1], ("zn",), 1),
        swap(halves[2], ("c",), 1),
        swap(halves[3], ("zn", "c"), 3),
    ]

    result = tangent_product(side, blocks, halves).reshape(slots, parts * 4, size)
    returned = spread(result)
    returned = returned.at[q_owner].get(mode="promise_in_bounds")
    return returned.reshape(slots, parts, 4, size).astype(jnp.float32)


def solution(mesh):
    split = Mesh(mesh.devices.reshape(2, 4, 4, 2, 2, 2), OWNER + ROW)
    return jax.shard_map(
        steps,
        mesh=split,
        in_specs=(P(OWNER, None, ROW, None), P(None, None, OWNER, ROW), P(), P(OWNER, None)),
        out_specs=P(None, None, ROW + OWNER, None),
        check_vma=False,
    )
```

profile of v0, /device:TPU:2, one launch (start us, length us, event | category | flops | bytes accessed | tf_op | source)
XLA Modules:
  0.0 150.9 jit_solution(15444247094179578828)
XLA Ops:
  0.0 0.0 copy-start
  0.0 0.8 select_reduce_fusion
  0.9 0.4 copy-done
  1.2 0.0 copy-start.2
  1.2 1.6 %gather_fusion = bf16[64,2,32,128]{3,2,1,0:T(8,128)(2,1)} fusion(bf16[64,2,32,128]{3,2,1,0:T(8,128)(2,1)S(1)} %copy-done, s32[1024]{0:T(1024)S(1)} %pad_clamp_fusion.1), kind=kCustom, calls=%fused_computation | custom fusion | bytes 2097408 | tf_op jit(solution)/shard_map/gather | solution.py:194
  2.9 0.0 copy-start.3
  2.9 15.0 %all-to-all-start = ((bf16[64,2,32,128]{3,2,1,0:T(8,128)(2,1)}), bf16[64,2,32,128]{3,2,1,0:T(8,128)(2,1)}, u32[]{:S(2)}, u32[]{:S(2)}) async-start(bf16[64,2,32,128]{3,2,1,0:T(8,128)(2,1)} %gather_fusion), calls=%async_computation | async-start | bytes 2097152 | tf_op jit(solution)/shard_map/all_to_all | solution.py:33
  17.9 0.0 copy-done.2
  17.9 0.9 dynamic-slice_bitcast_fusion
  18.8 2.4 %collective-permute-start = (bf16[2,128,1024]{2,1,0:T(8,128)(2,1)S(1)}, bf16[2,128,1024]{2,1,0:T(8,128)(2,1)}, u32[]{:S(2)}, u32[]{:S(2)}) collective-permute-start(bf16[2,128,1024]{2,1,0:T(8,128)(2,1)S(1)} %get-tuple-element.13), channel_id=1, source_target_pairs={{0,4},{4,0},{1,5},{5,1},{2,6},{6,2},{3,7},{7,3},{8,12},{12,8},{9,1... | collective-permute-start | bytes 1572872 | tf_op jit(solution)/shard_map/ppermute | solution.py:21
  21.2 1.0 collective-permute-start.1
  22.2 42.9 %collective-permute-done.refs_1_ = bf16[2,128,1024]{2,1,0:T(8,128)(2,1)} collective-permute-done((bf16[2,128,1024]{2,1,0:T(8,128)(2,1)S(1)}, bf16[2,128,1024]{2,1,0:T(8,128)(2,1)}, u32[]{:S(2)}, u32[]{:S(2)}) %collective-permute-start) | collective-permute-done | bytes 524320 | tf_op jit(solution)/shard_map/ppermute | solution.py:21
  65.1 0.0 collective-permute-start.2
  65.1 0.0 collective-permute-start.3
  65.1 0.5 collective-permute-start.4
  65.6 0.0 collective-permute-done.1.refs_2_
  65.6 0.0 collective-permute-start.5
  65.6 13.2 %collective-permute-done.2.refs_3_ = bf16[2,128,1024]{2,1,0:T(8,128)(2,1)} collective-permute-done((bf16[2,128,1024]{2,1,0:T(8,128)(2,1)}, bf16[2,128,1024]{2,1,0:T(8,128)(2,1)}, u32[]{:S(2)}, u32[]{:S(2)}) %collective-permute-start.2) | collective-permute-done | bytes 524320 | tf_op jit(solution)/shard_map/ppermute | solution.py:21
  78.8 0.0 collective-permute-start.6
  78.8 0.0 copy-done.3
  78.8 1.1 copy.6.table_ref
  79.8 0.0 copy-start.1
  79.8 1.0 copy-done.1
  80.9 0.4 order.1.order_ref
  81.3 0.0 collective-permute-done.3.refs_4_
  81.3 0.0 collective-permute-done.4.refs_5_
  81.3 0.0 collective-permute-done.5.refs_6_
  81.3 0.0 collective-permute-done.6.refs_7_
  81.3 0.0 all-to-all-done
  81.3 6.1 %half.1 = (bf16[2,2,128,256]{3,2,1,0:T(8,128)(2,1)S(1)}, bf16[2,2,128,256]{3,2,1,0:T(8,128)(2,1)S(1)}, bf16[2,2,128,256]{3,2,1,0:T(8,128)(2,1)S(1)}, bf16[2,2,128,256]{3,2,1,0:T(8,128)(2,1)S(1)}) custom-call(s32[1]{0:T(128)} %bitcast.side_ref, bf16[1024,1024]{1,0:T(8,128)(2,1)S(1)} %order.1.order_ref, bf16[32,2,2,32,128]{4,3,2,1,0:T(8,128)(2,1)} %bitcast.6.landed_ref, ...), custom_call_target="tpu_custom_call" | custom-call | flops 3221225472 | bytes 6291456 | tf_op jit(solution)/shard_map/half/pallas_call | solution.py:98
  87.5 0.4 collective-permute-start.7
  87.9 0.3 collective-permute-start.8
  88.2 1.5 %collective-permute-start.9 = (bf16[2,2,128,256]{3,2,1,0:T(8,128)(2,1)S(1)}, bf16[2,2,128,256]{3,2,1,0:T(8,128)(2,1)S(1)}, u32[]{:S(2)}, u32[]{:S(2)}) collective-permute-start(bf16[2,2,128,256]{3,2,1,0:T(8,128)(2,1)S(1)} %get-tuple-element.12), channel_id=1, source_target_pairs={{0,3},{1,2},{2,1},{3,0},{4,7},{5,6},{6,5},{7,4},{8,11},{9,10},{10,... | collective-permute-start | bytes 786440 | tf_op jit(solution)/shard_map/ppermute | solution.py:21
  89.7 7.0 %collective-permute-done.7.refs_9_ = bf16[2,2,128,256]{3,2,1,0:T(8,128)(2,1)S(1)} collective-permute-done((bf16[2,2,128,256]{3,2,1,0:T(8,128)(2,1)S(1)}, bf16[2,2,128,256]{3,2,1,0:T(8,128)(2,1)S(1)}, u32[]{:S(2)}, u32[]{:S(2)}) %collective-permute-start.7) | collective-permute-done | bytes 262176 | tf_op jit(solution)/shard_map/ppermute | solution.py:21
  96.8 0.0 collective-permute-done.8.refs_10_
  96.8 4.7 %collective-permute-done.9.refs_11_ = bf16[2,2,128,256]{3,2,1,0:T(8,128)(2,1)S(1)} collective-permute-done((bf16[2,2,128,256]{3,2,1,0:T(8,128)(2,1)S(1)}, bf16[2,2,128,256]{3,2,1,0:T(8,128)(2,1)S(1)}, u32[]{:S(2)}, u32[]{:S(2)}) %collective-permute-start.9) | collective-permute-done | bytes 262176 | tf_op jit(solution)/shard_map/ppermute | solution.py:21
  101.4 5.7 %tangent.1 = bf16[32,2,8,1024]{3,2,1,0:T(8,128)(2,1)} custom-call(s32[1]{0:T(128)} %bitcast.side_ref, bf16[2,128,1024]{2,1,0:T(8,128)(2,1)} %get-tuple-element.14.refs_0_, bf16[2,128,1024]{2,1,0:T(8,128)(2,1)} %collective-permute-done.refs_1_, bf16[2,128,1024]{2,1,0:T(8,128)(2,1)} %collective-permute-done.1.refs_2_, ...), custom_call_target="tpu_custom_call" | custom-call | flops 2147483648 | bytes 6291456 | tf_op jit(solution)/shard_map/tangent/pallas_call | solution.py:159
  107.2 0.0 copy-start.4
  107.2 11.3 %all-to-all-start.1 = ((bf16[64,8,1024]{2,1,0:T(8,128)(2,1)}), bf16[64,8,1024]{2,1,0:T(8,128)(2,1)S(1)}, u32[]{:S(2)}, u32[]{:S(2)}) async-start(bf16[64,8,1024]{2,1,0:T(8,128)(2,1)} %bitcast.7), calls=%async_computation.1 | async-start | bytes 2097152 | tf_op jit(solution)/shard_map/all_to_all | solution.py:33
  118.5 0.0 copy-done.4
  118.5 30.1 %all-to-all-done.1 = bf16[64,8,1024]{2,1,0:T(8,128)(2,1)S(1)} async-done(((bf16[64,8,1024]{2,1,0:T(8,128)(2,1)}), bf16[64,8,1024]{2,1,0:T(8,128)(2,1)S(1)}, u32[]{:S(2)}, u32[]{:S(2)}) %all-to-all-start.1) | async-done | bytes 1048608 | tf_op jit(solution)/shard_map/all_to_all | solution.py:33
  148.6 0.6 gather_fusion.1
  149.3 1.7 %reshape.26 = f32[64,2,4,1024]{3,2,1,0:T(4,128)} reshape(bf16[64,8,1024]{2,1,0:T(8,128)(2,1)S(1)} %gather_fusion.1) | data formatting | bytes 3145728 | tf_op jit(solution)/shard_map/convert_element_type | solution.py:213
  (5 shorter events, 0.0 us)
Async XLA Ops:
  0.0 1.2 copy-start
  1.2 16.6 %copy-start.2 = (bf16[2,2,128,1024]{3,2,1,0:T(8,128)(2,1)S(1)}, bf16[2,2,128,1024]{3,2,1,0:T(8,128)(2,1)}, u32[]{:S(2)}) copy-start(bf16[2,2,128,1024]{3,2,1,0:T(8,128)(2,1)} %param.4) | copy-start | bytes 3145732
  2.9 75.9 %copy-start.3 = (s32[2,1024]{1,0:T(2,128)S(1)}, s32[2,1024]{1,0:T(2,128)}, u32[]{:S(2)}) copy-start(s32[2,1024]{1,0:T(2,128)} %param.7) | copy-start | bytes 24580
  2.9 78.4 %all-to-all-start = ((bf16[64,2,32,128]{3,2,1,0:T(8,128)(2,1)}), bf16[64,2,32,128]{3,2,1,0:T(8,128)(2,1)}, u32[]{:S(2)}, u32[]{:S(2)}) async-start(bf16[64,2,32,128]{3,2,1,0:T(8,128)(2,1)} %gather_fusion), calls=%async_computation | async-start | bytes 2097152 | tf_op jit(solution)/shard_map/all_to_all | solution.py:33
  18.8 46.2 %collective-permute-start = (bf16[2,128,1024]{2,1,0:T(8,128)(2,1)S(1)}, bf16[2,128,1024]{2,1,0:T(8,128)(2,1)}, u32[]{:S(2)}, u32[]{:S(2)}) collective-permute-start(bf16[2,128,1024]{2,1,0:T(8,128)(2,1)S(1)} %get-tuple-element.13), channel_id=1, source_target_pairs={{0,4},{4,0},{1,5},{5,1},{2,6},{6,2},{3,7},{7,3},{8,12},{12,8},{9,1... | collective-permute-start | bytes 1572872 | tf_op jit(solution)/shard_map/ppermute | solution.py:21
  21.2 44.4 %collective-permute-start.1 = (bf16[2,128,1024]{2,1,0:T(8,128)(2,1)}, bf16[2,128,1024]{2,1,0:T(8,128)(2,1)}, u32[]{:S(2)}, u32[]{:S(2)}) collective-permute-start(bf16[2,128,1024]{2,1,0:T(8,128)(2,1)} %get-tuple-element.14.refs_0_), channel_id=1, source_target_pairs={{0,2},{2,0},{1,3},{3,1},{4,6},{6,4},{5,7},{7,5},{8,10},{10,8},{9,1... | collective-permute-start | bytes 1572872 | tf_op jit(solution)/shard_map/ppermute | solution.py:21
  65.1 13.7 %collective-permute-start.2 = (bf16[2,128,1024]{2,1,0:T(8,128)(2,1)}, bf16[2,128,1024]{2,1,0:T(8,128)(2,1)}, u32[]{:S(2)}, u32[]{:S(2)}) collective-permute-start(bf16[2,128,1024]{2,1,0:T(8,128)(2,1)} %collective-permute-done.refs_1_), channel_id=1, source_target_pairs={{0,2},{2,0},{1,3},{3,1},{4,6},{6,4},{5,7},{7,5},{8,10},{10,8},{9,1... | collective-permute-start | bytes 1572872 | tf_op jit(solution)/shard_map/ppermute | solution.py:21
  65.1 16.2 %collective-permute-start.3 = (bf16[2,128,1024]{2,1,0:T(8,128)(2,1)}, bf16[2,128,1024]{2,1,0:T(8,128)(2,1)}, u32[]{:S(2)}, u32[]{:S(2)}) collective-permute-start(bf16[2,128,1024]{2,1,0:T(8,128)(2,1)} %get-tuple-element.14.refs_0_), channel_id=1, source_target_pairs={{0,1},{1,0},{2,3},{3,2},{4,5},{5,4},{6,7},{7,6},{8,9},{9,8},{10,11... | collective-permute-start | bytes 1572872 | tf_op jit(solution)/shard_map/ppermute | solution.py:21
  65.1 16.2 %collective-permute-start.4 = (bf16[2,128,1024]{2,1,0:T(8,128)(2,1)}, bf16[2,128,1024]{2,1,0:T(8,128)(2,1)}, u32[]{:S(2)}, u32[]{:S(2)}) collective-permute-start(bf16[2,128,1024]{2,1,0:T(8,128)(2,1)} %collective-permute-done.refs_1_), channel_id=1, source_target_pairs={{0,1},{1,0},{2,3},{3,2},{4,5},{5,4},{6,7},{7,6},{8,9},{9,8},{10,11... | collective-permute-start | bytes 1572872 | tf_op jit(solution)/shard_map/ppermute | solution.py:21
  65.6 15.7 %collective-permute-start.5 = (bf16[2,128,1024]{2,1,0:T(8,128)(2,1)}, bf16[2,128,1024]{2,1,0:T(8,128)(2,1)}, u32[]{:S(2)}, u32[]{:S(2)}) collective-permute-start(bf16[2,128,1024]{2,1,0:T(8,128)(2,1)} %collective-permute-done.1.refs_2_), channel_id=1, source_target_pairs={{0,1},{1,0},{2,3},{3,2},{4,5},{5,4},{6,7},{7,6},{8,9},{9,8},{10,11... | collective-permute-start | bytes 1572872 | tf_op jit(solution)/shard_map/ppermute | solution.py:21
  78.8 2.6 %collective-permute-start.6 = (bf16[2,128,1024]{2,1,0:T(8,128)(2,1)}, bf16[2,128,1024]{2,1,0:T(8,128)(2,1)}, u32[]{:S(2)}, u32[]{:S(2)}) collective-permute-start(bf16[2,128,1024]{2,1,0:T(8,128)(2,1)} %collective-permute-done.2.refs_3_), channel_id=1, source_target_pairs={{0,1},{1,0},{2,3},{3,2},{4,5},{5,4},{6,7},{7,6},{8,9},{9,8},{10,11... | collective-permute-start | bytes 1572872 | tf_op jit(solution)/shard_map/ppermute | solution.py:21
  79.8 1.0 copy-start.1
  87.5 9.3 %collective-permute-start.7 = (bf16[2,2,128,256]{3,2,1,0:T(8,128)(2,1)S(1)}, bf16[2,2,128,256]{3,2,1,0:T(8,128)(2,1)S(1)}, u32[]{:S(2)}, u32[]{:S(2)}) collective-permute-start(bf16[2,2,128,256]{3,2,1,0:T(8,128)(2,1)S(1)} %get-tuple-element.10), channel_id=1, source_target_pairs={{0,2},{2,0},{1,3},{3,1},{4,6},{6,4},{5,7},{7,5},{8,10},{10,8},{9,1... | collective-permute-start | bytes 786440 | tf_op jit(solution)/shard_map/ppermute | solution.py:21
  87.9 8.9 %collective-permute-start.8 = (bf16[2,2,128,256]{3,2,1,0:T(8,128)(2,1)S(1)}, bf16[2,2,128,256]{3,2,1,0:T(8,128)(2,1)S(1)}, u32[]{:S(2)}, u32[]{:S(2)}) collective-permute-start(bf16[2,2,128,256]{3,2,1,0:T(8,128)(2,1)S(1)} %get-tuple-element.11), channel_id=1, source_target_pairs={{0,1},{1,0},{2,3},{3,2},{4,5},{5,4},{6,7},{7,6},{8,9},{9,8},{10,11... | collective-permute-start | bytes 786440 | tf_op jit(solution)/shard_map/ppermute | solution.py:21
  88.2 13.3 %collective-permute-start.9 = (bf16[2,2,128,256]{3,2,1,0:T(8,128)(2,1)S(1)}, bf16[2,2,128,256]{3,2,1,0:T(8,128)(2,1)S(1)}, u32[]{:S(2)}, u32[]{:S(2)}) collective-permute-start(bf16[2,2,128,256]{3,2,1,0:T(8,128)(2,1)S(1)} %get-tuple-element.12), channel_id=1, source_target_pairs={{0,3},{1,2},{2,1},{3,0},{4,7},{5,6},{6,5},{7,4},{8,11},{9,10},{10,... | collective-permute-start | bytes 786440 | tf_op jit(solution)/shard_map/ppermute | solution.py:21
  107.2 11.3 %copy-start.4 = (s32[64]{0:T(128)S(1)}, s32[64]{0:T(128)}, u32[]{:S(2)}) copy-start(s32[64]{0:T(128)} %param.6) | copy-start | bytes 772
  107.2 41.5 %all-to-all-start.1 = ((bf16[64,8,1024]{2,1,0:T(8,128)(2,1)}), bf16[64,8,1024]{2,1,0:T(8,128)(2,1)S(1)}, u32[]{:S(2)}, u32[]{:S(2)}) async-start(bf16[64,8,1024]{2,1,0:T(8,128)(2,1)} %bitcast.7), calls=%async_computation.1 | async-start | bytes 2097152 | tf_op jit(solution)/shard_map/all_to_all | solution.py:33
where the time goes:
time: 151 us
  waiting for transfers between devices  97.9 us (65%)
  starting transfers between devices  32.4 us (21%)
  Pallas kernels  12.2 us (8%)
  local copies, waits for them, and re-layouts  7.34 us (5%)
    ppermute x10, waiting for transfers between devices, swap(): return lax.ppermute(x, axes, [(i, i ^ mask) for i in range(count)])  67.8 us
    all_to_all x2, waiting for transfers between devices, spread(): return lax.all_to_all(x, SPREAD, 0, 0, tiled=True)  30.1 us
    all_to_all x2, starting transfers between devices, spread(): return lax.all_to_all(x, SPREAD, 0, 0, tiled=True)  26.3 us
    pallas_call x1, Pallas kernels, half_product(): pl.pallas_call(half_kernel, out_shape=[VMEM((2, 2, rows, 2 * width), jnp....  6.14 us
    ppermute x10, starting transfers between devices, swap(): return lax.ppermute(x, axes, [(i, i ^ mask) for i in range(count)])  6.13 us
    pallas_call x1, Pallas kernels, tangent_product(): pl.pallas_call(tangent_kernel, out_shape=VMEM((owners, 2, 8, size), jnp.b...  5.71 us
  transfers between devices with their start and end apart: 12, of which 5 were waited for; matrix products, arithmetic and copies ran while one was open for 1% of the time, Pallas kernels for 0%

commit v1 on v0

--- a/solution.py
+++ b/solution.py
@@ -54,9 +54,18 @@
     )(side, table)
 
 
-def half_kernel(side_ref, order_ref, landed_ref, *refs):
-    w_refs, outs = refs[:8], refs[8:12]
-    w, chi, w_sems, chi_sems = refs[12:]
+def half_block(w, k, both):
+    width = both.shape[1] // 2
+    real = jnp.dot(w[k, 0], both, preferred_element_type=jnp.float32)
+    imag = jnp.dot(w[k, 1], both, preferred_element_type=jnp.float32)
+    first = real[:, :width] - imag[:, width:]
+    second = real[:, width:] + imag[:, :width]
+    return first.astype(jnp.bfloat16), second.astype(jnp.bfloat16)
+
+
+def early_kernel(side_ref, order_ref, landed_ref, *refs):
+    w_refs, both_ref, own, cross, far_two, far_six = refs[:6], *refs[6:11]
+    w, chi, w_sems, chi_sems = refs[11:]
     width = landed_ref.shape[-1]
     side = side_ref[0]
     chi_copies, w_copies = [], []
@@ -70,7 +79,7 @@
                     chi_sems.at[at],
                 )
             )
-    for k in range(8):
+    for k in range(6):
         w_copies.append(pltpu.make_async_copy(w_refs[k], w.at[k], w_sems.at[k]))
     for copy in chi_copies + w_copies:
         copy.start()
@@ -79,44 +88,72 @@
         copy.wait()
     both = chi[...].reshape(size, 4 * width)
     both = jnp.dot(order_ref[...], both, preferred_element_type=jnp.float32)
-    real, imag = both[:, : 2 * width], both[:, 2 * width :]
-    first = both.astype(jnp.bfloat16)
-    second = jnp.concatenate([-imag, real], axis=1).astype(jnp.bfloat16)
-    for k in range(8):
+    both = both.astype(jnp.bfloat16)
+    both_ref[...] = both
+    outs = (far_two, far_six, own.at[0], own.at[1], cross.at[0], cross.at[1])
+    for k in range(6):
         w_copies[k].wait()
-        half = jnp.dot(w[k, 0], first, preferred_element_type=jnp.float32)
-        half += jnp.dot(w[k, 1], second, preferred_element_type=jnp.float32)
-        half = half.astype(jnp.bfloat16)
-        dm, delta = k % 2, k // 2
-        outs[delta][0, dm] = half[:, : 2 * width]
-        outs[delta][1, dm] = half[:, 2 * width :]
-
-
-def half_product(side, order, blocks, landed):
+        outs[k][0], outs[k][1] = half_block(w, k, both)
+
+
+def early_half(side, order, blocks, landed):
     rows, size = blocks[0].shape[1:]
     owners, _, _, short, width = landed.shape
-    return pl.pallas_call(
-        half_kernel,
-        out_shape=[VMEM((2, 2, rows, 2 * width), jnp.bfloat16)] * 4,
-        in_specs=[pl.BlockSpec(memory_space=pltpu.SMEM), DENSE] + [FAR] * 9,
-        out_specs=[DENSE] * 4,
+    one = VMEM((2, rows, 2 * width), jnp.bfloat16)
+    two = VMEM((2, 2, rows, 2 * width), jnp.bfloat16)
+    return pl.pallas_call(
+        early_kernel,
+        out_shape=[VMEM((size, 4 * width), jnp.bfloat16), two, two, one, one],
+        in_specs=[pl.BlockSpec(memory_space=pltpu.SMEM), DENSE] + [FAR] * 7,
+        out_specs=[DENSE] * 5,
         scratch_shapes=[
-            pltpu.VMEM((8, 2, rows, size), jnp.bfloat16),
+            pltpu.VMEM((6, 2, rows, size), jnp.bfloat16),
             pltpu.VMEM((owners, short, 4 * width), jnp.bfloat16),
-            pltpu.SemaphoreType.DMA((8,)),
+            pltpu.SemaphoreType.DMA((6,)),
             pltpu.SemaphoreType.DMA((4,)),
         ],
         compiler_params=PARAMS,
         cost_estimate=pl.CostEstimate(
-            flops=2 * size * size * 4 * width * 3, bytes_accessed=6 * 2**20, transcendentals=0
+            flops=5 * size * size * 4 * width, bytes_accessed=5 * 2**20, transcendentals=0
         ),
-        name="half",
+        name="early",
     )(side, *near([order]), *far([landed, *blocks]))
 
 
+def late_kernel(both_ref, w_ref, v_ref, one_ref, two_ref, w, sems):
+    copies = [
+        pltpu.make_async_copy(ref, w.at[k], sems.at[k]) for k, ref in enumerate((w_ref, v_ref))
+    ]
+    for copy in copies:
+        copy.start()
+    for k, out in enumerate((one_ref, two_ref)):
+        copies[k].wait()
+        out[0], out[1] = half_block(w, k, both_ref[...])
+
+
+def late_half(both, blocks):
+    rows, size = blocks[0].shape[1:]
+    one = VMEM((2, rows, both.shape[1] // 2), jnp.bfloat16)
+    return pl.pallas_call(
+        late_kernel,
+        out_shape=[one, one],
+        in_specs=[DENSE, FAR, FAR],
+        out_specs=[DENSE] * 2,
+        scratch_shapes=[
+            pltpu.VMEM((2, 2, rows, size), jnp.bfloat16),
+            pltpu.SemaphoreType.DMA((2,)),
+        ],
+        compiler_params=PARAMS,
+        cost_estimate=pl.CostEstimate(
+            flops=8 * rows * size * both.shape[1], bytes_accessed=2 * 2**20, transcendentals=0
+        ),
+        name="late",
+    )(*near([both]), *far(blocks))
+
+
 def tangent_kernel(side_ref, *refs):
-    w_refs, h_refs, out_ref = refs[:8], refs[8:12], refs[12]
-    w, mixed, w_sems = refs[13:]
+    w_refs, h_refs, out_ref = refs[:8], refs[8:14], refs[14]
+    w, mixed, w_sems = refs[15:]
     rows, size = w.shape[2:]
     copies = []
     for k in range(8):
@@ -128,7 +165,15 @@
             )
     for copy in copies:
         copy.start()
-    left = jnp.concatenate([h[...].reshape(4 * rows, 2 * rows) for h in h_refs], axis=1)
+    own, cross, *far_ones = h_refs
+    pairs = ((own.at[0], own.at[1]), far_ones[:2], (cross.at[0], cross.at[1]), far_ones[2:])
+    left = jnp.concatenate(
+        [
+            jnp.concatenate([h[part] for part in range(2) for h in pair], axis=0)
+            for pair in pairs
+        ],
+        axis=1,
+    )
     for copy in copies:
         copy.wait()
     side = side_ref[0]
@@ -159,7 +204,7 @@
     return pl.pallas_call(
         tangent_kernel,
         out_shape=VMEM((owners, 2, 8, size), jnp.bfloat16),
-        in_specs=[pl.BlockSpec(memory_space=pltpu.SMEM)] + [FAR] * 8 + [DENSE] * 4,
+        in_specs=[pl.BlockSpec(memory_space=pltpu.SMEM)] + [FAR] * 8 + [DENSE] * 6,
         out_specs=DENSE,
         scratch_shapes=[
             pltpu.VMEM((2, 8, rows, size), jnp.bfloat16),
@@ -184,8 +229,10 @@
     def pick(x, k):
         return lax.dynamic_index_in_dim(x, k, 0, keepdims=False)
 
+    outgoing = pick(screened, 1 - zm)
+    other = swap(outgoing, ("zm",), 1)
+    screened, _ = lax.optimization_barrier((screened, outgoing))
     mine = pick(screened, zm)
-    other = swap(pick(screened, 1 - zm), ("zm",), 1)
     across = [swap(mine, ("zn",), 1)]
     order = order_matrix(side, pick(g_index, zm)[:, None])
 
@@ -197,15 +244,18 @@
 
     across.append(swap(other, ("zn",), 1))
     blocks = [mine, other] + across
-    blocks += [swap(block, ("c",), 1) for block in blocks]
-
-    halves = half_product(side, order, blocks, landed)
-    halves = [
-        halves[0],
-        swap(halves[1], ("zn",), 1),
-        swap(halves[2], ("c",), 1),
-        swap(halves[3], ("zn", "c"), 3),
-    ]
+    blocks += [swap(block, ("c",), 1) for block in blocks[:3]]
+    blocks.append(swap(blocks[3], ("c",), 1))
+
+    ready = [blocks[k] for k in (2, 6, 0, 1, 4, 5)]
+    both, own, cross, zn_first, far_first = early_half(side, order, ready, landed)
+    zn_first = swap(zn_first, ("zn",), 1)
+    far_first = swap(far_first, ("zn", "c"), 3)
+    cross = swap(cross, ("c",), 1)
+    zn_last, far_last = late_half(both, [blocks[3], blocks[7]])
+    zn_last = swap(zn_last, ("zn",), 1)
+    far_last = swap(far_last, ("zn", "c"), 3)
+    halves = [own, cross, zn_first, zn_last, far_first, far_last]
 
     result = tangent_product(side, blocks, halves).reshape(slots, parts * 4, size)
     returned = spread(result)

time: 151 us -> 153 us (1.013)
  starting transfers between devices: 32.4 us -> 34.5 us
    ppermute x10 -> x12, starting transfers between devices: 6.13 us -> 8.22 us  [swap(): return lax.ppermute(x, axes, [(i, i ^ mask) for i in range(count)])]
    ppermute x10 -> x12, waiting for transfers between devices: 67.8 us -> 66.6 us  [swap(): return lax.ppermute(x, axes, [(i, i ^ mask) for i in range(count)])]
    pallas_call x1 -> x2, Pallas kernels: 6.14 us -> 7.19 us  [the longest x1 5.23 us: early_half(): pl.pallas_call(early_kernel, out_shape=[VMEM((size, 4 * width), jnp.bfloa...]
  transfers between devices with their start and end apart: 12 -> 14, of which waited for: 5 -> 7; matrix products, arithmetic and copies ran while one was open for 1% -> 1% of each run, Pallas kernels for 0% -> 5%
where the time goes in v1:
time: 153 us
  waiting for transfers between devices  96.4 us (63%)
  starting transfers between devices  34.5 us (23%)
  Pallas kernels  13.3 us (9%)
  local copies, waits for them, and re-layouts  7.29 us (5%)
    ppermute x12, waiting for transfers between devices, swap(): return lax.ppermute(x, axes, [(i, i ^ mask) for i in range(count)])  66.6 us
    all_to_all x2, waiting for transfers between devices, spread(): return lax.all_to_all(x, SPREAD, 0, 0, tiled=True)  29.8 us
    all_to_all x2, starting transfers between devices, spread(): return lax.all_to_all(x, SPREAD, 0, 0, tiled=True)  26.3 us
    ppermute x12, starting transfers between devices, swap(): return lax.ppermute(x, axes, [(i, i ^ mask) for i in range(count)])  8.22 us
    pallas_call x1, Pallas kernels, tangent_product(): pl.pallas_call(tangent_kernel, out_shape=VMEM((owners, 2, 8, size), jnp.b...  5.71 us
    pallas_call x1, Pallas kernels, early_half(): pl.pallas_call(early_kernel, out_shape=[VMEM((size, 4 * width), jnp.bfloa...  5.23 us
  transfers between devices with their start and end apart: 14, of which 7 were waited for; matrix products, arithmetic and copies ran while one was open for 1% of the time, Pallas kernels for 5%

profile of v1, /device:TPU:2, one launch (start us, length us, event | category | flops | bytes accessed | tf_op | source)
XLA Modules:
  0.0 152.5 jit_solution(6731070509206373805)
XLA Ops:
  0.0 0.0 copy-start
  0.0 0.8 select_reduce_fusion
  0.9 0.4 copy-done
  1.2 0.0 copy-start.2
  1.2 1.6 %gather_fusion = bf16[64,2,32,128]{3,2,1,0:T(8,128)(2,1)} fusion(bf16[64,2,32,128]{3,2,1,0:T(8,128)(2,1)S(1)} %copy-done, s32[1024]{0:T(1024)S(1)} %pad_clamp_fusion.1), kind=kCustom, calls=%fused_computation | custom fusion | bytes 2097408 | tf_op jit(solution)/shard_map/gather | solution.py:241
  2.9 0.0 copy-start.3
  2.9 15.0 %all-to-all-start = ((bf16[64,2,32,128]{3,2,1,0:T(8,128)(2,1)}), bf16[64,2,32,128]{3,2,1,0:T(8,128)(2,1)}, u32[]{:S(2)}, u32[]{:S(2)}) async-start(bf16[64,2,32,128]{3,2,1,0:T(8,128)(2,1)} %gather_fusion), calls=%async_computation | async-start | bytes 2097152 | tf_op jit(solution)/shard_map/all_to_all | solution.py:33
  17.9 0.0 copy-done.2
  17.9 2.4 %collective-permute-start = (bf16[2,128,1024]{2,1,0:T(8,128)(2,1)S(1)}, bf16[2,128,1024]{2,1,0:T(8,128)(2,1)}, u32[]{:S(2)}, u32[]{:S(2)}) collective-permute-start(bf16[2,128,1024]{2,1,0:T(8,128)(2,1)S(1)} %dynamic-slice_bitcast_fusion.1), channel_id=1, source_target_pairs={{0,4},{4,0},{1,5},{5,1},{2,6},{6,2},{3,7},{7,3},{8,12},{12,8},{9,1... | collective-permute-start | bytes 1572872 | tf_op jit(solution)/shard_map/ppermute | solution.py:21
  20.4 0.8 dynamic-slice_bitcast_fusion.refs_2_.refs_0_
  21.2 1.0 collective-permute-start.1
  22.3 42.8 %collective-permute-done.refs_3_.refs_1_ = bf16[2,128,1024]{2,1,0:T(8,128)(2,1)} collective-permute-done((bf16[2,128,1024]{2,1,0:T(8,128)(2,1)S(1)}, bf16[2,128,1024]{2,1,0:T(8,128)(2,1)}, u32[]{:S(2)}, u32[]{:S(2)}) %collective-permute-start) | collective-permute-done | bytes 524320 | tf_op jit(solution)/shard_map/ppermute | solution.py:21
  65.1 0.0 collective-permute-start.2
  65.1 0.0 collective-permute-start.3
  65.1 0.0 collective-permute-done.1.refs_0_.refs_2_
  65.1 0.5 collective-permute-start.5
  65.6 0.1 collective-permute-start.4
  65.7 13.1 %collective-permute-done.2.w_ref.refs_3_ = bf16[2,128,1024]{2,1,0:T(8,128)(2,1)} collective-permute-done((bf16[2,128,1024]{2,1,0:T(8,128)(2,1)}, bf16[2,128,1024]{2,1,0:T(8,128)(2,1)}, u32[]{:S(2)}, u32[]{:S(2)}) %collective-permute-start.2) | collective-permute-done | bytes 524320 | tf_op jit(solution)/shard_map/ppermute | solution.py:21
  78.8 0.0 collective-permute-start.6
  78.8 0.0 copy-done.3
  78.8 1.0 copy.6.table_ref
  79.8 0.0 copy-start.1
  79.8 1.0 copy-done.1
  80.9 0.4 order.1.order_ref
  81.3 0.0 collective-permute-done.3.refs_4_
  81.3 0.0 collective-permute-done.5.refs_1_.refs_6_
  81.3 0.0 collective-permute-done.4.refs_5_
  81.3 0.0 all-to-all-done
  81.3 5.2 %early.1 = (bf16[1024,512]{1,0:T(8,128)(2,1)S(1)}, bf16[2,2,128,256]{3,2,1,0:T(8,128)(2,1)S(1)}, bf16[2,2,128,256]{3,2,1,0:T(8,128)(2,1)S(1)}, bf16[2,128,256]{2,1,0:T(8,128)(2,1)S(1)}, bf16[2,128,256]{2,1,0:T(8,128)(2,1)S(1)}) custom-call(s32[1]{0:T(128)} %bitcast.side_ref, bf16[1024,1024]{1,0:T(8,128)(2,1)S(1)} %order.1.order_ref, ...), custom_call_target="tpu_custom_call" | custom-call | flops 2684354560 | bytes 5242880 | tf_op jit(solution)/shard_map/early/pallas_call | solution.py:104
  86.6 0.6 collective-permute-start.7
  87.1 0.0 collective-permute-done.6.v_ref.refs_7_
  87.1 2.0 %late.1 = (bf16[2,128,256]{2,1,0:T(8,128)(2,1)S(1)}, bf16[2,128,256]{2,1,0:T(8,128)(2,1)S(1)}) custom-call(bf16[1024,512]{1,0:T(8,128)(2,1)S(1)} %get-tuple-element.17.both_ref, bf16[2,128,1024]{2,1,0:T(8,128)(2,1)} %collective-permute-done.2.w_ref.refs_3_, bf16[2,128,1024]{2,1,0:T(8,128)(2,1)} %collective-permute-done.6.v_ref.refs_7_), custom_call_target="tpu_custom_call" | custom-call | flops 536870912 | bytes 2097152 | tf_op jit(solution)/shard_map/late/pallas_call | solution.py:137
  89.1 0.1 collective-permute-start.11
  89.2 1.6 %collective-permute-start.9 = (bf16[2,128,256]{2,1,0:T(8,128)(2,1)S(1)}, bf16[2,128,256]{2,1,0:T(8,128)(2,1)S(1)}, u32[]{:S(2)}, u32[]{:S(2)}) collective-permute-start(bf16[2,128,256]{2,1,0:T(8,128)(2,1)S(1)} %get-tuple-element.18), channel_id=1, source_target_pairs={{0,2},{2,0},{1,3},{3,1},{4,6},{6,4},{5,7},{7,5},{8,10},{10,8},{9,1... | collective-permute-start | bytes 393224 | tf_op jit(solution)/shard_map/ppermute | solution.py:21
  90.9 0.1 collective-permute-start.10
  91.0 1.7 %collective-permute-start.8 = (bf16[2,128,256]{2,1,0:T(8,128)(2,1)S(1)}, bf16[2,128,256]{2,1,0:T(8,128)(2,1)S(1)}, u32[]{:S(2)}, u32[]{:S(2)}) collective-permute-start(bf16[2,128,256]{2,1,0:T(8,128)(2,1)S(1)} %get-tuple-element.16), channel_id=1, source_target_pairs={{0,2},{2,0},{1,3},{3,1},{4,6},{6,4},{5,7},{7,5},{8,10},{10,8},{9,1... | collective-permute-start | bytes 393224 | tf_op jit(solution)/shard_map/ppermute | solution.py:21
  92.7 2.1 %collective-permute-done.11.refs_13_ = bf16[2,128,256]{2,1,0:T(8,128)(2,1)S(1)} collective-permute-done((bf16[2,128,256]{2,1,0:T(8,128)(2,1)S(1)}, bf16[2,128,256]{2,1,0:T(8,128)(2,1)S(1)}, u32[]{:S(2)}, u32[]{:S(2)}) %collective-permute-start.11) | collective-permute-done | bytes 131104 | tf_op jit(solution)/shard_map/ppermute | solution.py:21
  94.8 3.2 %collective-permute-done.9.refs_11_ = bf16[2,128,256]{2,1,0:T(8,128)(2,1)S(1)} collective-permute-done((bf16[2,128,256]{2,1,0:T(8,128)(2,1)S(1)}, bf16[2,128,256]{2,1,0:T(8,128)(2,1)S(1)}, u32[]{:S(2)}, u32[]{:S(2)}) %collective-permute-start.9) | collective-permute-done | bytes 131104 | tf_op jit(solution)/shard_map/ppermute | solution.py:21
  98.0 2.4 %collective-permute-done.10.refs_12_ = bf16[2,128,256]{2,1,0:T(8,128)(2,1)S(1)} collective-permute-done((bf16[2,128,256]{2,1,0:T(8,128)(2,1)S(1)}, bf16[2,128,256]{2,1,0:T(8,128)(2,1)S(1)}, u32[]{:S(2)}, u32[]{:S(2)}) %collective-permute-start.10) | collective-permute-done | bytes 131104 | tf_op jit(solution)/shard_map/ppermute | solution.py:21
  100.4 3.0 %collective-permute-done.8.refs_10_ = bf16[2,128,256]{2,1,0:T(8,128)(2,1)S(1)} collective-permute-done((bf16[2,128,256]{2,1,0:T(8,128)(2,1)S(1)}, bf16[2,128,256]{2,1,0:T(8,128)(2,1)S(1)}, u32[]{:S(2)}, u32[]{:S(2)}) %collective-permute-start.8) | collective-permute-done | bytes 131104 | tf_op jit(solution)/shard_map/ppermute | solution.py:21
  103.4 0.0 collective-permute-done.7.refs_9_
  103.4 5.7 %tangent.1 = bf16[32,2,8,1024]{3,2,1,0:T(8,128)(2,1)} custom-call(s32[1]{0:T(128)} %bitcast.side_ref, bf16[2,128,1024]{2,1,0:T(8,128)(2,1)} %dynamic-slice_bitcast_fusion.refs_2_.refs_0_, bf16[2,128,1024]{2,1,0:T(8,128)(2,1)} %collective-permute-done.refs_3_.refs_1_, bf16[2,128,1024]{2,1,0:T(8,128)(2,1)} %collective-permute-done.1.refs_0_.refs_2_, ...), custom_call_target="tpu_custom_call" | custom-call | flops 2147483648 | bytes 6291456 | tf_op jit(solution)/shard_map/tangent/pallas_call | solution.py:204
  109.1 0.0 copy-start.4
  109.2 11.3 %all-to-all-start.1 = ((bf16[64,8,1024]{2,1,0:T(8,128)(2,1)}), bf16[64,8,1024]{2,1,0:T(8,128)(2,1)S(1)}, u32[]{:S(2)}, u32[]{:S(2)}) async-start(bf16[64,8,1024]{2,1,0:T(8,128)(2,1)} %bitcast.7), calls=%async_computation.1 | async-start | bytes 2097152 | tf_op jit(solution)/shard_map/all_to_all | solution.py:33
  120.5 0.0 copy-done.4
  120.5 29.8 %all-to-all-done.1 = bf16[64,8,1024]{2,1,0:T(8,128)(2,1)S(1)} async-done(((bf16[64,8,1024]{2,1,0:T(8,128)(2,1)}), bf16[64,8,1024]{2,1,0:T(8,128)(2,1)S(1)}, u32[]{:S(2)}, u32[]{:S(2)}) %all-to-all-start.1) | async-done | bytes 1048608 | tf_op jit(solution)/shard_map/all_to_all | solution.py:33
  150.3 0.6 gather_fusion.1
  150.9 1.7 %reshape.26 = f32[64,2,4,1024]{3,2,1,0:T(4,128)} reshape(bf16[64,8,1024]{2,1,0:T(8,128)(2,1)S(1)} %gather_fusion.1) | data formatting | bytes 3145728 | tf_op jit(solution)/shard_map/convert_element_type | solution.py:263
  (6 shorter events, 0.1 us)
Async XLA Ops:
  0.0 1.2 copy-start
  1.2 16.6 %copy-start.2 = (bf16[2,2,128,1024]{3,2,1,0:T(8,128)(2,1)S(1)}, bf16[2,2,128,1024]{3,2,1,0:T(8,128)(2,1)}, u32[]{:S(2)}) copy-start(bf16[2,2,128,1024]{3,2,1,0:T(8,128)(2,1)} %param.4) | copy-start | bytes 3145732
  2.9 75.9 %copy-start.3 = (s32[2,1024]{1,0:T(2,128)S(1)}, s32[2,1024]{1,0:T(2,128)}, u32[]{:S(2)}) copy-start(s32[2,1024]{1,0:T(2,128)} %param.7) | copy-start | bytes 24580
  2.9 78.4 %all-to-all-start = ((bf16[64,2,32,128]{3,2,1,0:T(8,128)(2,1)}), bf16[64,2,32,128]{3,2,1,0:T(8,128)(2,1)}, u32[]{:S(2)}, u32[]{:S(2)}) async-start(bf16[64,2,32,128]{3,2,1,0:T(8,128)(2,1)} %gather_fusion), calls=%async_computation | async-start | bytes 2097152 | tf_op jit(solution)/shard_map/all_to_all | solution.py:33
  17.9 47.1 %collective-permute-start = (bf16[2,128,1024]{2,1,0:T(8,128)(2,1)S(1)}, bf16[2,128,1024]{2,1,0:T(8,128)(2,1)}, u32[]{:S(2)}, u32[]{:S(2)}) collective-permute-start(bf16[2,128,1024]{2,1,0:T(8,128)(2,1)S(1)} %dynamic-slice_bitcast_fusion.1), channel_id=1, source_target_pairs={{0,4},{4,0},{1,5},{5,1},{2,6},{6,2},{3,7},{7,3},{8,12},{12,8},{9,1... | collective-permute-start | bytes 1572872 | tf_op jit(solution)/shard_map/ppermute | solution.py:21
  21.2 43.8 %collective-permute-start.1 = (bf16[2,128,1024]{2,1,0:T(8,128)(2,1)}, bf16[2,128,1024]{2,1,0:T(8,128)(2,1)}, u32[]{:S(2)}, u32[]{:S(2)}) collective-permute-start(bf16[2,128,1024]{2,1,0:T(8,128)(2,1)} %dynamic-slice_bitcast_fusion.refs_2_.refs_0_), channel_id=1, source_target_pairs={{0,2},{2,0},{1,3},{3,1},{4,6},{6,4},{5,7},{7,5},{8,10},{10,8},{9,1... | collective-permute-start | bytes 1572872 | tf_op jit(solution)/shard_map/ppermute | solution.py:21
  65.1 13.7 %collective-permute-start.2 = (bf16[2,128,1024]{2,1,0:T(8,128)(2,1)}, bf16[2,128,1024]{2,1,0:T(8,128)(2,1)}, u32[]{:S(2)}, u32[]{:S(2)}) collective-permute-start(bf16[2,128,1024]{2,1,0:T(8,128)(2,1)} %collective-permute-done.refs_3_.refs_1_), channel_id=1, source_target_pairs={{0,2},{2,0},{1,3},{3,1},{4,6},{6,4},{5,7},{7,5},{8,10},{10,8},{9,1... | collective-permute-start | bytes 1572872 | tf_op jit(solution)/shard_map/ppermute | solution.py:21
  65.1 16.2 %collective-permute-start.3 = (bf16[2,128,1024]{2,1,0:T(8,128)(2,1)}, bf16[2,128,1024]{2,1,0:T(8,128)(2,1)}, u32[]{:S(2)}, u32[]{:S(2)}) collective-permute-start(bf16[2,128,1024]{2,1,0:T(8,128)(2,1)} %dynamic-slice_bitcast_fusion.refs_2_.refs_0_), channel_id=1, source_target_pairs={{0,1},{1,0},{2,3},{3,2},{4,5},{5,4},{6,7},{7,6},{8,9},{9,8},{10,11... | collective-permute-start | bytes 1572872 | tf_op jit(solution)/shard_map/ppermute | solution.py:21
  65.1 16.2 %collective-permute-start.5 = (bf16[2,128,1024]{2,1,0:T(8,128)(2,1)}, bf16[2,128,1024]{2,1,0:T(8,128)(2,1)}, u32[]{:S(2)}, u32[]{:S(2)}) collective-permute-start(bf16[2,128,1024]{2,1,0:T(8,128)(2,1)} %collective-permute-done.1.refs_0_.refs_2_), channel_id=1, source_target_pairs={{0,1},{1,0},{2,3},{3,2},{4,5},{5,4},{6,7},{7,6},{8,9},{9,8},{10,11... | collective-permute-start | bytes 1572872 | tf_op jit(solution)/shard_map/ppermute | solution.py:21
  65.6 15.7 %collective-permute-start.4 = (bf16[2,128,1024]{2,1,0:T(8,128)(2,1)}, bf16[2,128,1024]{2,1,0:T(8,128)(2,1)}, u32[]{:S(2)}, u32[]{:S(2)}) collective-permute-start(bf16[2,128,1024]{2,1,0:T(8,128)(2,1)} %collective-permute-done.refs_3_.refs_1_), channel_id=1, source_target_pairs={{0,1},{1,0},{2,3},{3,2},{4,5},{5,4},{6,7},{7,6},{8,9},{9,8},{10,11... | collective-permute-start | bytes 1572872 | tf_op jit(solution)/shard_map/ppermute | solution.py:21
  78.8 8.4 %collective-permute-start.6 = (bf16[2,128,1024]{2,1,0:T(8,128)(2,1)}, bf16[2,128,1024]{2,1,0:T(8,128)(2,1)}, u32[]{:S(2)}, u32[]{:S(2)}) collective-permute-start(bf16[2,128,1024]{2,1,0:T(8,128)(2,1)} %collective-permute-done.2.w_ref.refs_3_), channel_id=1, source_target_pairs={{0,1},{1,0},{2,3},{3,2},{4,5},{5,4},{6,7},{7,6},{8,9},{9,8},{10,11... | collective-permute-start | bytes 1572872 | tf_op jit(solution)/shard_map/ppermute | solution.py:21
  79.8 1.0 copy-start.1
  86.6 16.9 %collective-permute-start.7 = (bf16[2,2,128,256]{3,2,1,0:T(8,128)(2,1)S(1)}, bf16[2,2,128,256]{3,2,1,0:T(8,128)(2,1)S(1)}, u32[]{:S(2)}, u32[]{:S(2)}) collective-permute-start(bf16[2,2,128,256]{3,2,1,0:T(8,128)(2,1)S(1)} %get-tuple-element.15), channel_id=1, source_target_pairs={{0,1},{1,0},{2,3},{3,2},{4,5},{5,4},{6,7},{7,6},{8,9},{9,8},{10,11... | collective-permute-start | bytes 786440 | tf_op jit(solution)/shard_map/ppermute | solution.py:21
  89.1 5.7 %collective-permute-start.11 = (bf16[2,128,256]{2,1,0:T(8,128)(2,1)S(1)}, bf16[2,128,256]{2,1,0:T(8,128)(2,1)S(1)}, u32[]{:S(2)}, u32[]{:S(2)}) collective-permute-start(bf16[2,128,256]{2,1,0:T(8,128)(2,1)S(1)} %get-tuple-element.20), channel_id=1, source_target_pairs={{0,3},{1,2},{2,1},{3,0},{4,7},{5,6},{6,5},{7,4},{8,11},{9,10},{10,... | collective-permute-start | bytes 393224 | tf_op jit(solution)/shard_map/ppermute | solution.py:21
  89.2 8.8 %collective-permute-start.9 = (bf16[2,128,256]{2,1,0:T(8,128)(2,1)S(1)}, bf16[2,128,256]{2,1,0:T(8,128)(2,1)S(1)}, u32[]{:S(2)}, u32[]{:S(2)}) collective-permute-start(bf16[2,128,256]{2,1,0:T(8,128)(2,1)S(1)} %get-tuple-element.18), channel_id=1, source_target_pairs={{0,2},{2,0},{1,3},{3,1},{4,6},{6,4},{5,7},{7,5},{8,10},{10,8},{9,1... | collective-permute-start | bytes 393224 | tf_op jit(solution)/shard_map/ppermute | solution.py:21
  90.9 9.6 %collective-permute-start.10 = (bf16[2,128,256]{2,1,0:T(8,128)(2,1)S(1)}, bf16[2,128,256]{2,1,0:T(8,128)(2,1)S(1)}, u32[]{:S(2)}, u32[]{:S(2)}) collective-permute-start(bf16[2,128,256]{2,1,0:T(8,128)(2,1)S(1)} %get-tuple-element.19), channel_id=1, source_target_pairs={{0,3},{1,2},{2,1},{3,0},{4,7},{5,6},{6,5},{7,4},{8,11},{9,10},{10,... | collective-permute-start | bytes 393224 | tf_op jit(solution)/shard_map/ppermute | solution.py:21
  91.0 12.5 %collective-permute-start.8 = (bf16[2,128,256]{2,1,0:T(8,128)(2,1)S(1)}, bf16[2,128,256]{2,1,0:T(8,128)(2,1)S(1)}, u32[]{:S(2)}, u32[]{:S(2)}) collective-permute-start(bf16[2,128,256]{2,1,0:T(8,128)(2,1)S(1)} %get-tuple-element.16), channel_id=1, source_target_pairs={{0,2},{2,0},{1,3},{3,1},{4,6},{6,4},{5,7},{7,5},{8,10},{10,8},{9,1... | collective-permute-start | bytes 393224 | tf_op jit(solution)/shard_map/ppermute | solution.py:21
  109.1 11.3 %copy-start.4 = (s32[64]{0:T(128)S(1)}, s32[64]{0:T(128)}, u32[]{:S(2)}) copy-start(s32[64]{0:T(128)} %param.6) | copy-start | bytes 772
  109.2 41.1 %all-to-all-start.1 = ((bf16[64,8,1024]{2,1,0:T(8,128)(2,1)}), bf16[64,8,1024]{2,1,0:T(8,128)(2,1)S(1)}, u32[]{:S(2)}, u32[]{:S(2)}) async-start(bf16[64,8,1024]{2,1,0:T(8,128)(2,1)} %bitcast.7), calls=%async_computation.1 | async-start | bytes 2097152 | tf_op jit(solution)/shard_map/all_to_all | solution.py:33

commit v2 on v1

v2 whole, which is shorter than its diff:
```python
import jax
import jax.numpy as jnp
from jax import lax
from jax.experimental import pallas as pl
from jax.experimental.pallas import tpu as pltpu
from jax.sharding import Mesh, PartitionSpec as P


OWNER = ("zh", "y", "x")
ROW = ("zm", "zn", "c")
SPREAD = ("zh", "y", "x", "zm")

FAR = pl.BlockSpec(memory_space=pltpu.MemorySpace.HBM)
DENSE = pl.BlockSpec(memory_space=pltpu.VMEM)
VMEM = pltpu.VMEM
PARAMS = pltpu.CompilerParams(vmem_limit_bytes=32 * 2**20)


def swap(x, axes, mask):
    count = 2 ** len(axes)
    return lax.ppermute(x, axes, [(i, i ^ mask) for i in range(count)])


def near(xs):
    return [pltpu.with_memory_space_constraint(x, pltpu.VMEM) for x in xs]


def far(xs):
    return [pltpu.with_memory_space_constraint(x, pltpu.MemorySpace.HBM) for x in xs]


def spread(x):
    return lax.all_to_all(x, SPREAD, 0, 0, tiled=True)


def order_kernel(side_ref, table_ref, out_ref):
    size = out_ref.shape[0]
    step = 128
    for i in range(0, size, step):
        ids = lax.broadcasted_iota(jnp.int32, (step, size), 1)
        hit = ids == table_ref[i : i + step, :]
        out_ref[i : i + step, :] = jnp.where(hit, 1.0, 0.0).astype(jnp.bfloat16)


def order_matrix(side, table):
    size = table.shape[0]
    return pl.pallas_call(
        order_kernel,
        out_shape=VMEM((size, size), jnp.bfloat16),
        in_specs=[pl.BlockSpec(memory_space=pltpu.SMEM), DENSE],
        out_specs=DENSE,
        compiler_params=PARAMS,
        name="order",
    )(side, table)


def half_block(w, k, both):
    width = both.shape[1] // 2
    real = jnp.dot(w[0, k], both, preferred_element_type=jnp.float32)
    imag = jnp.dot(w[1, k], both, preferred_element_type=jnp.float32)
    first = real[:, :width] - imag[:, width:]
    second = real[:, width:] + imag[:, :width]
    return first.astype(jnp.bfloat16), second.astype(jnp.bfloat16)


def early_kernel(side_ref, order_ref, landed_ref, *refs):
    w_refs, both_ref, own, cross, w = refs[:4], *refs[4:8]
    chi, w_sems, chi_sems = refs[8:]
    width = landed_ref.shape[-1]
    side = side_ref[0]
    chi_copies, w_copies = [], []
    for b in range(2):
        for part in range(2):
            at = part * 2 + b
            chi_copies.append(
                pltpu.make_async_copy(
                    landed_ref.at[:, side ^ b, part],
                    chi.at[:, :, pl.ds(at * width, width)],
                    chi_sems.at[at],
                )
            )
    for k in range(4):
        w_copies.append(pltpu.make_async_copy(w_refs[k], w.at[:, k], w_sems.at[k]))
    for copy in chi_copies + w_copies:
        copy.start()
    size = order_ref.shape[0]
    for copy in chi_copies:
        copy.wait()
    both = chi[...].reshape(size, 4 * width)
    both = jnp.dot(order_ref[...], both, preferred_element_type=jnp.float32)
    both = both.astype(jnp.bfloat16)
    both_ref[...] = both
    outs = (own.at[0], own.at[1], cross.at[0], cross.at[1])
    for k in range(4):
        w_copies[k].wait()
        outs[k][0], outs[k][1] = half_block(w, k, both)


def early_half(side, order, blocks, landed):
    rows, size = blocks[0].shape[1:]
    owners, _, _, short, width = landed.shape
    two = VMEM((2, 2, rows, 2 * width), jnp.bfloat16)
    return pl.pallas_call(
        early_kernel,
        out_shape=[VMEM((size, 4 * width), jnp.bfloat16), two, two]
        + [VMEM((2, 4, rows, size), jnp.bfloat16)],
        in_specs=[pl.BlockSpec(memory_space=pltpu.SMEM), DENSE] + [FAR] * 5,
        out_specs=[DENSE] * 4,
        scratch_shapes=[
            pltpu.VMEM((owners, short, 4 * width), jnp.bfloat16),
            pltpu.SemaphoreType.DMA((4,)),
            pltpu.SemaphoreType.DMA((4,)),
        ],
        compiler_params=PARAMS,
        cost_estimate=pl.CostEstimate(
            flops=4 * size * size * 4 * width, bytes_accessed=5 * 2**20, transcendentals=0
        ),
        name="early",
    )(side, *near([order]), *far([landed, *blocks]))


def pair_kernel(both_ref, w_ref, v_ref, one_ref, two_ref, w, sems):
    copies = [
        pltpu.make_async_copy(ref, w.at[:, k], sems.at[k]) for k, ref in enumerate((w_ref, v_ref))
    ]
    for copy in copies:
        copy.start()
    for k, out in enumerate((one_ref, two_ref)):
        copies[k].wait()
        out[0], out[1] = half_block(w, k, both_ref[...])


def pair_half(both, blocks):
    rows, size = blocks[0].shape[1:]
    one = VMEM((2, rows, both.shape[1] // 2), jnp.bfloat16)
    return pl.pallas_call(
        pair_kernel,
        out_shape=[one, one, VMEM((2, 2, rows, size), jnp.bfloat16)],
        in_specs=[DENSE, FAR, DENSE],
        out_specs=[DENSE] * 3,
        scratch_shapes=[pltpu.SemaphoreType.DMA((2,))],
        compiler_params=PARAMS,
        cost_estimate=pl.CostEstimate(
            flops=8 * rows * size * both.shape[1], bytes_accessed=2 * 2**20, transcendentals=0
        ),
    )(*near([both]), *far(blocks[:1]), *near(blocks[1:]))


def tangent_kernel(side_ref, four, first_two, last_two, *refs):
    (own, cross, zn_first, zn_last, far_first, far_last), out_ref = refs[:6], refs[6]
    mixed = refs[7]
    rows, size = four.shape[2:]
    owners = out_ref.shape[0]
    wide = size // 2

    def stacked(first, last):
        return jnp.concatenate([h[part] for part in range(2) for h in (first, last)], axis=0)

    zn, distant = stacked(zn_first, zn_last), stacked(far_first, far_last)
    lefts = (
        jnp.concatenate([stacked(h.at[0], h.at[1]) for h in (own, cross)], axis=1),
        jnp.concatenate([zn[:, :rows], distant[:, :rows]], axis=1),
        jnp.concatenate([zn[:, rows:], distant[:, rows:]], axis=1),
    )
    for h in range(2):
        lanes = slice(h * wide, h * wide + wide)

        def by(part):
            total = 0.0
            for left, w in zip(lefts, (four, first_two, last_two)):
                right = w[part, :, :, lanes].reshape(left.shape[1], wide)
                total += jnp.dot(left, right, preferred_element_type=jnp.float32)
            return total

        by_real, by_imag = by(0), by(1)
        cut = 2 * rows
        real = by_real[:cut] - by_imag[cut:]
        imag = by_imag[:cut] + by_real[cut:]
        for j in range(2 * owners):
            mixed[j, 0:4, :] = real[4 * j : 4 * j + 4, :]
            mixed[j, 4:8, :] = imag[4 * j : 4 * j + 4, :]
        for b in range(2):
            piece = mixed[b * owners : (b + 1) * owners].astype(jnp.bfloat16)
            out_ref[:, side_ref[0] ^ b, :, lanes] = piece


def tangent_product(side, weights, halves):
    rows, size = weights[0].shape[2:]
    owners = rows // 4
    return pl.pallas_call(
        tangent_kernel,
        out_shape=jax.ShapeDtypeStruct((owners, 2, 8, size), jnp.bfloat16),
        in_specs=[pl.BlockSpec(memory_space=pltpu.SMEM)] + [DENSE] * 9,
        out_specs=DENSE,
        scratch_shapes=[pltpu.VMEM((2 * owners, 8, size // 2), jnp.float32)],
        compiler_params=PARAMS,
        cost_estimate=pl.CostEstimate(
            flops=2 * 4 * rows * size * size * 2, bytes_accessed=3 * 2**20, transcendentals=0
        ),
        name="tangent",
    )(side, *near([*weights, *halves]))


def steps(screened, response, q_owner, g_index):
    slots = q_owner.shape[0]
    _, parts, _, size = screened.shape
    short, width = response.shape[2:]
    zm = lax.axis_index("zm")
    side = zm[None].astype(jnp.int32)

    def pick(x, k):
        return lax.dynamic_index_in_dim(x, k, 0, keepdims=False)

    outgoing = pick(screened, 1 - zm)
    other = swap(outgoing, ("zm",), 1)
    screened, _ = lax.optimization_barrier((screened, outgoing))
    mine = pick(screened, zm)
    across = [swap(mine, ("zn",), 1)]
    order = order_matrix(side, pick(g_index, zm)[:, None])

    ids = jnp.arange(slots, dtype=jnp.int32)
    inverse = jnp.sum(jnp.where(q_owner[None, :] == ids[:, None], ids[None, :], 0), axis=1)
    ordered = response.at[inverse].get(mode="promise_in_bounds")
    landed = spread(ordered)
    landed = landed.reshape(slots // 2, 2, parts, short, width)

    across.append(swap(other, ("zn",), 1))
    blocks = [mine, other] + across
    blocks += [swap(block, ("c",), 1) for block in blocks[:2]]
    blocks.append(swap(blocks[2], ("c",), 1))
    blocks.append(swap(blocks[3], ("c",), 1))

    ready = [blocks[k] for k in (0, 1, 4, 5)]
    both, own, cross, four = early_half(side, order, ready, landed)
    zn_first, far_first, first_two = pair_half(both, [blocks[2], blocks[6]])
    zn_first = swap(zn_first, ("zn",), 1)
    far_first = swap(far_first, ("zn", "c"), 3)
    cross = swap(cross, ("c",), 1)
    zn_last, far_last, last_two = pair_half(both, [blocks[3], blocks[7]])
    zn_last = swap(zn_last, ("zn",), 1)
    far_last = swap(far_last, ("zn", "c"), 3)
    halves = [own, cross, zn_first, zn_last, far_first, far_last]

    result = tangent_product(side, (four, first_two, last_two), halves)
    returned = spread(result.reshape(slots, parts * 4, size))
    returned = returned.at[q_owner].get(mode="promise_in_bounds")
    return returned.reshape(slots, parts, 4, size).astype(jnp.float32)


def solution(mesh):
    split = Mesh(mesh.devices.reshape(2, 4, 4, 2, 2, 2), OWNER + ROW)
    return jax.shard_map(
        steps,
        mesh=split,
        in_specs=(P(OWNER, None, ROW, None), P(None, None, OWNER, ROW), P(), P(OWNER, None)),
        out_specs=P(None, None, ROW + OWNER, None),
        check_vma=False,
    )
```

time: 153 us -> 162 us (1.059)
  waiting for transfers between devices: 96.4 us -> 103 us
    ppermute x12, waiting for transfers between devices: 66.6 us -> 73.9 us  [swap(): return lax.ppermute(x, axes, [(i, i ^ mask) for i in range(count)])]
    pallas_call x2 -> x3, Pallas kernels: 7.67 us -> 9.45 us  [the longest x2 6.01 us: pair_half(): pl.pallas_call(pair_kernel, out_shape=[one, one, VMEM((2, 2, rows, size),...]
  transfers between devices with their start and end apart: 14 -> 14, of which waited for: 7 -> 7; matrix products, arithmetic and copies ran while one was open for 1% -> 1% of each run, Pallas kernels for 5% -> 7%
where the time goes in v2:
time: 162 us; the launch traced here: 161 us
  waiting for transfers between devices  103 us (64%)
  starting transfers between devices  35.6 us (22%)
  Pallas kernels  14.2 us (9%)
  local copies, waits for them, and re-layouts  7.25 us (4%)
    ppermute x12, waiting for transfers between devices, swap(): return lax.ppermute(x, axes, [(i, i ^ mask) for i in range(count)])  73.9 us
    all_to_all x2, waiting for transfers between devices, spread(): return lax.all_to_all(x, SPREAD, 0, 0, tiled=True)  29.3 us
    all_to_all x2, starting transfers between devices, spread(): return lax.all_to_all(x, SPREAD, 0, 0, tiled=True)  26.3 us
    ppermute x12, starting transfers between devices, swap(): return lax.ppermute(x, axes, [(i, i ^ mask) for i in range(count)])  9.24 us
    pallas_call x2, Pallas kernels, pair_half(): pl.pallas_call(pair_kernel, out_shape=[one, one, VMEM((2, 2, rows, size),...  6.01 us
    pallas_call x1, Pallas kernels, early_half(): pl.pallas_call(early_kernel, out_shape=[VMEM((size, 4 * width), jnp.bfloa...  4.34 us
    pallas_call x1, Pallas kernels, tangent_product(): pl.pallas_call(tangent_kernel, out_shape=jax.ShapeDtypeStruct((owners, 2,...  3.43 us
  transfers between devices with their start and end apart: 14, of which 7 were waited for; matrix products, arithmetic and copies ran while one was open for 1% of the time, Pallas kernels for 7%

profile of v2, /device:TPU:2, one launch (start us, length us, event | category | flops | bytes accessed | tf_op | source)
XLA Modules:
  0.0 161.2 jit_solution(2967611951344777608)
XLA Ops:
  0.0 0.0 copy-start
  0.0 0.8 select_reduce_fusion
  0.9 0.4 copy-done
  1.2 0.0 copy-start.2
  1.2 1.6 %gather_fusion = bf16[64,2,32,128]{3,2,1,0:T(8,128)(2,1)} fusion(bf16[64,2,32,128]{3,2,1,0:T(8,128)(2,1)S(1)} %copy-done, s32[1024]{0:T(1024)S(1)} %pad_clamp_fusion.1), kind=kCustom, calls=%fused_computation | custom fusion | bytes 2097408 | tf_op jit(solution)/shard_map/gather | solution.py:223
  2.9 0.0 copy-start.3
  2.9 15.0 %all-to-all-start = ((bf16[64,2,32,128]{3,2,1,0:T(8,128)(2,1)}), bf16[64,2,32,128]{3,2,1,0:T(8,128)(2,1)}, u32[]{:S(2)}, u32[]{:S(2)}) async-start(bf16[64,2,32,128]{3,2,1,0:T(8,128)(2,1)} %gather_fusion), calls=%async_computation | async-start | bytes 2097152 | tf_op jit(solution)/shard_map/all_to_all | solution.py:33
  17.9 0.0 copy-done.2
  17.9 2.4 %collective-permute-start = (bf16[2,128,1024]{2,1,0:T(8,128)(2,1)S(1)}, bf16[2,128,1024]{2,1,0:T(8,128)(2,1)}, u32[]{:S(2)}, u32[]{:S(2)}) collective-permute-start(bf16[2,128,1024]{2,1,0:T(8,128)(2,1)S(1)} %dynamic-slice_bitcast_fusion.1), channel_id=1, source_target_pairs={{0,4},{4,0},{1,5},{5,1},{2,6},{6,2},{3,7},{7,3},{8,12},{12,8},{9,1... | collective-permute-start | bytes 1572872 | tf_op jit(solution)/shard_map/ppermute | solution.py:21
  20.4 44.7 %collective-permute-done.refs_1_ = bf16[2,128,1024]{2,1,0:T(8,128)(2,1)} collective-permute-done((bf16[2,128,1024]{2,1,0:T(8,128)(2,1)S(1)}, bf16[2,128,1024]{2,1,0:T(8,128)(2,1)}, u32[]{:S(2)}, u32[]{:S(2)}) %collective-permute-start) | collective-permute-done | bytes 524320 | tf_op jit(solution)/shard_map/ppermute | solution.py:21
  65.1 0.0 collective-permute-start.5
  65.1 0.8 dynamic-slice_bitcast_fusion.refs_0_
  65.9 2.0 %collective-permute-start.3 = (bf16[2,128,1024]{2,1,0:T(8,128)(2,1)}, bf16[2,128,1024]{2,1,0:T(8,128)(2,1)}, u32[]{:S(2)}, u32[]{:S(2)}) collective-permute-start(bf16[2,128,1024]{2,1,0:T(8,128)(2,1)} %dynamic-slice_bitcast_fusion.refs_0_), channel_id=1, source_target_pairs={{0,2},{2,0},{1,3},{3,1},{4,6},{6,4},{5,7},{7,5},{8,10},{10,8},{9,1... | collective-permute-start | bytes 1572872 | tf_op jit(solution)/shard_map/ppermute | solution.py:21
  67.9 0.0 collective-permute-start.1
  67.9 0.5 collective-permute-start.2
  68.4 11.8 %collective-permute-done.5.w_ref = bf16[2,128,1024]{2,1,0:T(8,128)(2,1)} collective-permute-done((bf16[2,128,1024]{2,1,0:T(8,128)(2,1)}, bf16[2,128,1024]{2,1,0:T(8,128)(2,1)}, u32[]{:S(2)}, u32[]{:S(2)}) %collective-permute-start.5) | collective-permute-done | bytes 524320 | tf_op jit(solution)/shard_map/ppermute | solution.py:21
  80.2 0.0 collective-permute-start.6
  80.2 9.8 %collective-permute-done.3.w_ref = bf16[2,128,1024]{2,1,0:T(8,128)(2,1)} collective-permute-done((bf16[2,128,1024]{2,1,0:T(8,128)(2,1)}, bf16[2,128,1024]{2,1,0:T(8,128)(2,1)}, u32[]{:S(2)}, u32[]{:S(2)}) %collective-permute-start.3) | collective-permute-done | bytes 524320 | tf_op jit(solution)/shard_map/ppermute | solution.py:21
  90.0 0.0 collective-permute-start.4
  90.0 0.0 copy-done.3
  90.0 1.0 copy.6.table_ref
  91.1 0.0 copy-start.1
  91.1 1.0 copy-done.1
  92.1 0.4 order.1.order_ref
  92.5 0.0 collective-permute-done.1.refs_2_
  92.5 0.0 collective-permute-done.2.refs_3_
  92.5 0.0 all-to-all-done
  92.5 4.3 %early.1 = (bf16[1024,512]{1,0:T(8,128)(2,1)S(1)}, bf16[2,2,128,256]{3,2,1,0:T(8,128)(2,1)S(1)}, bf16[2,2,128,256]{3,2,1,0:T(8,128)(2,1)S(1)}, bf16[2,4,128,1024]{3,2,1,0:T(8,128)(2,1)S(1)}) custom-call(s32[1]{0:T(128)} %bitcast.side_ref, bf16[1024,1024]{1,0:T(8,128)(2,1)S(1)} %order.1.order_ref, bf16[32,2,2,32,128]{4,3,2,1,0:T(8,128)(2,1)} %bitcast.4.landed_ref, ...), custom_call_target="tpu_custom_call" | custom-call | flops 2147483648 | bytes 5242880 | tf_op jit(solution)/shard_map/early/pallas_call | solution.py:103
  96.9 0.6 collective-permute-start.7
  97.5 0.0 collective-permute-done.6.v_ref
  97.5 3.0 %shard_map.47 = (bf16[2,128,256]{2,1,0:T(8,128)(2,1)S(1)}, bf16[2,128,256]{2,1,0:T(8,128)(2,1)S(1)}, bf16[2,2,128,1024]{3,2,1,0:T(8,128)(2,1)S(1)}) custom-call(bf16[1024,512]{1,0:T(8,128)(2,1)S(1)} %get-tuple-element.18.both_ref, bf16[2,128,1024]{2,1,0:T(8,128)(2,1)} %collective-permute-done.5.w_ref, bf16[2,128,1024]{2,1,0:T(8,128)(2,1)} %collective-permute-done.6.v_ref), custom_call_target="tpu_custom_call" | custom-call | flops 536870912 | bytes 2097152 | tf_op jit(solution)/shard_map/pallas_call | solution.py:136
  100.5 0.1 collective-permute-start.11
  100.6 1.6 %collective-permute-start.9 = (bf16[2,128,256]{2,1,0:T(8,128)(2,1)S(1)}, bf16[2,128,256]{2,1,0:T(8,128)(2,1)S(1)}, u32[]{:S(2)}, u32[]{:S(2)}) collective-permute-start(bf16[2,128,256]{2,1,0:T(8,128)(2,1)S(1)} %get-tuple-element.24), channel_id=1, source_target_pairs={{0,2},{2,0},{1,3},{3,1},{4,6},{6,4},{5,7},{7,5},{8,10},{10,8},{9,1... | collective-permute-start | bytes 393224 | tf_op jit(solution)/shard_map/ppermute | solution.py:21
  102.3 0.0 collective-permute-done.4.v_ref
  102.3 3.0 %shard_map.46 = (bf16[2,128,256]{2,1,0:T(8,128)(2,1)S(1)}, bf16[2,128,256]{2,1,0:T(8,128)(2,1)S(1)}, bf16[2,2,128,1024]{3,2,1,0:T(8,128)(2,1)S(1)}) custom-call(bf16[1024,512]{1,0:T(8,128)(2,1)S(1)} %get-tuple-element.18.both_ref, bf16[2,128,1024]{2,1,0:T(8,128)(2,1)} %collective-permute-done.3.w_ref, bf16[2,128,1024]{2,1,0:T(8,128)(2,1)} %collective-permute-done.4.v_ref), custom_call_target="tpu_custom_call" | custom-call | flops 536870912 | bytes 2097152 | tf_op jit(solution)/shard_map/pallas_call | solution.py:136
  105.3 0.2 collective-permute-start.10
  105.4 1.7 %collective-permute-start.8 = (bf16[2,128,256]{2,1,0:T(8,128)(2,1)S(1)}, bf16[2,128,256]{2,1,0:T(8,128)(2,1)S(1)}, u32[]{:S(2)}, u32[]{:S(2)}) collective-permute-start(bf16[2,128,256]{2,1,0:T(8,128)(2,1)S(1)} %get-tuple-element.23), channel_id=1, source_target_pairs={{0,2},{2,0},{1,3},{3,1},{4,6},{6,4},{5,7},{7,5},{8,10},{10,8},{9,1... | collective-permute-start | bytes 393224 | tf_op jit(solution)/shard_map/ppermute | solution.py:21
  107.2 0.0 collective-permute-done.11.refs_5_
  107.2 2.2 %collective-permute-done.9.refs_3_ = bf16[2,128,256]{2,1,0:T(8,128)(2,1)S(1)} collective-permute-done((bf16[2,128,256]{2,1,0:T(8,128)(2,1)S(1)}, bf16[2,128,256]{2,1,0:T(8,128)(2,1)S(1)}, u32[]{:S(2)}, u32[]{:S(2)}) %collective-permute-start.9) | collective-permute-done | bytes 131104 | tf_op jit(solution)/shard_map/ppermute | solution.py:21
  109.4 2.4 %collective-permute-done.10.refs_4_ = bf16[2,128,256]{2,1,0:T(8,128)(2,1)S(1)} collective-permute-done((bf16[2,128,256]{2,1,0:T(8,128)(2,1)S(1)}, bf16[2,128,256]{2,1,0:T(8,128)(2,1)S(1)}, u32[]{:S(2)}, u32[]{:S(2)}) %collective-permute-start.10) | collective-permute-done | bytes 131104 | tf_op jit(solution)/shard_map/ppermute | solution.py:21
  111.8 3.0 %collective-permute-done.8.refs_2_ = bf16[2,128,256]{2,1,0:T(8,128)(2,1)S(1)} collective-permute-done((bf16[2,128,256]{2,1,0:T(8,128)(2,1)S(1)}, bf16[2,128,256]{2,1,0:T(8,128)(2,1)S(1)}, u32[]{:S(2)}, u32[]{:S(2)}) %collective-permute-start.8) | collective-permute-done | bytes 131104 | tf_op jit(solution)/shard_map/ppermute | solution.py:21
  114.8 0.0 collective-permute-done.7.refs_1_
  114.8 3.4 %tangent.1 = bf16[32,2,8,1024]{3,2,1,0:T(8,128)(2,1)} custom-call(s32[1]{0:T(128)} %bitcast.side_ref, bf16[2,4,128,1024]{3,2,1,0:T(8,128)(2,1)S(1)} %get-tuple-element.17.four, bf16[2,2,128,1024]{3,2,1,0:T(8,128)(2,1)S(1)} %get-tuple-element.19.first_two, bf16[2,2,128,1024]{3,2,1,0:T(8,128)(2,1)S(1)} %get-tuple-element.20.last_two, ...), custom_call_target="tpu_custom_call" | custom-call | flops 2147483648 | bytes 3145728 | tf_op jit(solution)/shard_map/tangent/pallas_call | solution.py:190
  118.3 11.4 %all-to-all-start.1 = ((bf16[64,8,1024]{2,1,0:T(8,128)(2,1)}), bf16[64,8,1024]{2,1,0:T(8,128)(2,1)S(1)}, u32[]{:S(2)}, u32[]{:S(2)}) async-start(bf16[64,8,1024]{2,1,0:T(8,128)(2,1)} %bitcast.7), calls=%async_computation.1 | async-start | bytes 2097152 | tf_op jit(solution)/shard_map/all_to_all | solution.py:33
  129.6 0.0 copy-done.4
  129.7 29.3 %all-to-all-done.1 = bf16[64,8,1024]{2,1,0:T(8,128)(2,1)S(1)} async-done(((bf16[64,8,1024]{2,1,0:T(8,128)(2,1)}), bf16[64,8,1024]{2,1,0:T(8,128)(2,1)S(1)}, u32[]{:S(2)}, u32[]{:S(2)}) %all-to-all-start.1) | async-done | bytes 1048608 | tf_op jit(solution)/shard_map/all_to_all | solution.py:33
  158.9 0.6 gather_fusion.1
  159.5 1.7 %reshape.26 = f32[64,2,4,1024]{3,2,1,0:T(4,128)} reshape(bf16[64,8,1024]{2,1,0:T(8,128)(2,1)S(1)} %gather_fusion.1) | data formatting | bytes 3145728 | tf_op jit(solution)/shard_map/convert_element_type | solution.py:247
  (7 shorter events, 0.1 us)
Async XLA Ops:
  0.0 1.2 copy-start
  1.2 16.6 %copy-start.2 = (bf16[2,2,128,1024]{3,2,1,0:T(8,128)(2,1)S(1)}, bf16[2,2,128,1024]{3,2,1,0:T(8,128)(2,1)}, u32[]{:S(2)}) copy-start(bf16[2,2,128,1024]{3,2,1,0:T(8,128)(2,1)} %param.4) | copy-start | bytes 3145732
  2.9 87.1 %copy-start.3 = (s32[2,1024]{1,0:T(2,128)S(1)}, s32[2,1024]{1,0:T(2,128)}, u32[]{:S(2)}) copy-start(s32[2,1024]{1,0:T(2,128)} %param.7) | copy-start | bytes 24580
  2.9 89.6 %all-to-all-start = ((bf16[64,2,32,128]{3,2,1,0:T(8,128)(2,1)}), bf16[64,2,32,128]{3,2,1,0:T(8,128)(2,1)}, u32[]{:S(2)}, u32[]{:S(2)}) async-start(bf16[64,2,32,128]{3,2,1,0:T(8,128)(2,1)} %gather_fusion), calls=%async_computation | async-start | bytes 2097152 | tf_op jit(solution)/shard_map/all_to_all | solution.py:33
  17.9 47.1 %collective-permute-start = (bf16[2,128,1024]{2,1,0:T(8,128)(2,1)S(1)}, bf16[2,128,1024]{2,1,0:T(8,128)(2,1)}, u32[]{:S(2)}, u32[]{:S(2)}) collective-permute-start(bf16[2,128,1024]{2,1,0:T(8,128)(2,1)S(1)} %dynamic-slice_bitcast_fusion.1), channel_id=1, source_target_pairs={{0,4},{4,0},{1,5},{5,1},{2,6},{6,2},{3,7},{7,3},{8,12},{12,8},{9,1... | collective-permute-start | bytes 1572872 | tf_op jit(solution)/shard_map/ppermute | solution.py:21
  65.1 15.1 %collective-permute-start.5 = (bf16[2,128,1024]{2,1,0:T(8,128)(2,1)}, bf16[2,128,1024]{2,1,0:T(8,128)(2,1)}, u32[]{:S(2)}, u32[]{:S(2)}) collective-permute-start(bf16[2,128,1024]{2,1,0:T(8,128)(2,1)} %collective-permute-done.refs_1_), channel_id=1, source_target_pairs={{0,2},{2,0},{1,3},{3,1},{4,6},{6,4},{5,7},{7,5},{8,10},{10,8},{9,1... | collective-permute-start | bytes 1572872 | tf_op jit(solution)/shard_map/ppermute | solution.py:21
  65.9 24.1 %collective-permute-start.3 = (bf16[2,128,1024]{2,1,0:T(8,128)(2,1)}, bf16[2,128,1024]{2,1,0:T(8,128)(2,1)}, u32[]{:S(2)}, u32[]{:S(2)}) collective-permute-start(bf16[2,128,1024]{2,1,0:T(8,128)(2,1)} %dynamic-slice_bitcast_fusion.refs_0_), channel_id=1, source_target_pairs={{0,2},{2,0},{1,3},{3,1},{4,6},{6,4},{5,7},{7,5},{8,10},{10,8},{9,1... | collective-permute-start | bytes 1572872 | tf_op jit(solution)/shard_map/ppermute | solution.py:21
  67.9 24.6 %collective-permute-start.1 = (bf16[2,128,1024]{2,1,0:T(8,128)(2,1)}, bf16[2,128,1024]{2,1,0:T(8,128)(2,1)}, u32[]{:S(2)}, u32[]{:S(2)}) collective-permute-start(bf16[2,128,1024]{2,1,0:T(8,128)(2,1)} %dynamic-slice_bitcast_fusion.refs_0_), channel_id=1, source_target_pairs={{0,1},{1,0},{2,3},{3,2},{4,5},{5,4},{6,7},{7,6},{8,9},{9,8},{10,11... | collective-permute-start | bytes 1572872 | tf_op jit(solution)/shard_map/ppermute | solution.py:21
  67.9 24.6 %collective-permute-start.2 = (bf16[2,128,1024]{2,1,0:T(8,128)(2,1)}, bf16[2,128,1024]{2,1,0:T(8,128)(2,1)}, u32[]{:S(2)}, u32[]{:S(2)}) collective-permute-start(bf16[2,128,1024]{2,1,0:T(8,128)(2,1)} %collective-permute-done.refs_1_), channel_id=1, source_target_pairs={{0,1},{1,0},{2,3},{3,2},{4,5},{5,4},{6,7},{7,6},{8,9},{9,8},{10,11... | collective-permute-start | bytes 1572872 | tf_op jit(solution)/shard_map/ppermute | solution.py:21
  80.2 17.3 %collective-permute-start.6 = (bf16[2,128,1024]{2,1,0:T(8,128)(2,1)}, bf16[2,128,1024]{2,1,0:T(8,128)(2,1)}, u32[]{:S(2)}, u32[]{:S(2)}) collective-permute-start(bf16[2,128,1024]{2,1,0:T(8,128)(2,1)} %collective-permute-done.5.w_ref), channel_id=1, source_target_pairs={{0,1},{1,0},{2,3},{3,2},{4,5},{5,4},{6,7},{7,6},{8,9},{9,8},{10,11... | collective-permute-start | bytes 1572872 | tf_op jit(solution)/shard_map/ppermute | solution.py:21
  90.0 12.3 %collective-permute-start.4 = (bf16[2,128,1024]{2,1,0:T(8,128)(2,1)}, bf16[2,128,1024]{2,1,0:T(8,128)(2,1)}, u32[]{:S(2)}, u32[]{:S(2)}) collective-permute-start(bf16[2,128,1024]{2,1,0:T(8,128)(2,1)} %collective-permute-done.3.w_ref), channel_id=1, source_target_pairs={{0,1},{1,0},{2,3},{3,2},{4,5},{5,4},{6,7},{7,6},{8,9},{9,8},{10,11... | collective-permute-start | bytes 1572872 | tf_op jit(solution)/shard_map/ppermute | solution.py:21
  91.1 1.0 copy-start.1
  96.9 17.9 %collective-permute-start.7 = (bf16[2,2,128,256]{3,2,1,0:T(8,128)(2,1)S(1)}, bf16[2,2,128,256]{3,2,1,0:T(8,128)(2,1)S(1)}, u32[]{:S(2)}, u32[]{:S(2)}) collective-permute-start(bf16[2,2,128,256]{3,2,1,0:T(8,128)(2,1)S(1)} %get-tuple-element.22), channel_id=1, source_target_pairs={{0,1},{1,0},{2,3},{3,2},{4,5},{5,4},{6,7},{7,6},{8,9},{9,8},{10,11... | collective-permute-start | bytes 786440 | tf_op jit(solution)/shard_map/ppermute | solution.py:21
  100.5 6.7 %collective-permute-start.11 = (bf16[2,128,256]{2,1,0:T(8,128)(2,1)S(1)}, bf16[2,128,256]{2,1,0:T(8,128)(2,1)S(1)}, u32[]{:S(2)}, u32[]{:S(2)}) collective-permute-start(bf16[2,128,256]{2,1,0:T(8,128)(2,1)S(1)} %get-tuple-element.26), channel_id=1, source_target_pairs={{0,3},{1,2},{2,1},{3,0},{4,7},{5,6},{6,5},{7,4},{8,11},{9,10},{10,... | collective-permute-start | bytes 393224 | tf_op jit(solution)/shard_map/ppermute | solution.py:21
  100.6 8.8 %collective-permute-start.9 = (bf16[2,128,256]{2,1,0:T(8,128)(2,1)S(1)}, bf16[2,128,256]{2,1,0:T(8,128)(2,1)S(1)}, u32[]{:S(2)}, u32[]{:S(2)}) collective-permute-start(bf16[2,128,256]{2,1,0:T(8,128)(2,1)S(1)} %get-tuple-element.24), channel_id=1, source_target_pairs={{0,2},{2,0},{1,3},{3,1},{4,6},{6,4},{5,7},{7,5},{8,10},{10,8},{9,1... | collective-permute-start | bytes 393224 | tf_op jit(solution)/shard_map/ppermute | solution.py:21
  105.3 6.5 %collective-permute-start.10 = (bf16[2,128,256]{2,1,0:T(8,128)(2,1)S(1)}, bf16[2,128,256]{2,1,0:T(8,128)(2,1)S(1)}, u32[]{:S(2)}, u32[]{:S(2)}) collective-permute-start(bf16[2,128,256]{2,1,0:T(8,128)(2,1)S(1)} %get-tuple-element.25), channel_id=1, source_target_pairs={{0,3},{1,2},{2,1},{3,0},{4,7},{5,6},{6,5},{7,4},{8,11},{9,10},{10,... | collective-permute-start | bytes 393224 | tf_op jit(solution)/shard_map/ppermute | solution.py:21
  105.4 9.4 %collective-permute-start.8 = (bf16[2,128,256]{2,1,0:T(8,128)(2,1)S(1)}, bf16[2,128,256]{2,1,0:T(8,128)(2,1)S(1)}, u32[]{:S(2)}, u32[]{:S(2)}) collective-permute-start(bf16[2,128,256]{2,1,0:T(8,128)(2,1)S(1)} %get-tuple-element.23), channel_id=1, source_target_pairs={{0,2},{2,0},{1,3},{3,1},{4,6},{6,4},{5,7},{7,5},{8,10},{10,8},{9,1... | collective-permute-start | bytes 393224 | tf_op jit(solution)/shard_map/ppermute | solution.py:21
  118.3 11.4 %copy-start.4 = (s32[64]{0:T(128)S(1)}, s32[64]{0:T(128)}, u32[]{:S(2)}) copy-start(s32[64]{0:T(128)} %param.6) | copy-start | bytes 772
  118.3 40.7 %all-to-all-start.1 = ((bf16[64,8,1024]{2,1,0:T(8,128)(2,1)}), bf16[64,8,1024]{2,1,0:T(8,128)(2,1)S(1)}, u32[]{:S(2)}, u32[]{:S(2)}) async-start(bf16[64,8,1024]{2,1,0:T(8,128)(2,1)} %bitcast.7), calls=%async_computation.1 | async-start | bytes 2097152 | tf_op jit(solution)/shard_map/all_to_all | solution.py:33

commit v3 on v2

--- a/solution.py
+++ b/solution.py
@@ -64,8 +64,8 @@
 
 
 def early_kernel(side_ref, order_ref, landed_ref, *refs):
-    w_refs, both_ref, own, cross, w = refs[:4], *refs[4:8]
-    chi, w_sems, chi_sems = refs[8:]
+    w_refs, both_ref, own, cross, far_two, far_six, w = refs[:6], *refs[6:12]
+    chi, w_sems, chi_sems = refs[12:]
     width = landed_ref.shape[-1]
     side = side_ref[0]
     chi_copies, w_copies = [], []
@@ -79,7 +79,7 @@
                     chi_sems.at[at],
                 )
             )
-    for k in range(4):
+    for k in range(6):
         w_copies.append(pltpu.make_async_copy(w_refs[k], w.at[:, k], w_sems.at[k]))
     for copy in chi_copies + w_copies:
         copy.start()
@@ -90,8 +90,8 @@
     both = jnp.dot(order_ref[...], both, preferred_element_type=jnp.float32)
     both = both.astype(jnp.bfloat16)
     both_ref[...] = both
-    outs = (own.at[0], own.at[1], cross.at[0], cross.at[1])
-    for k in range(4):
+    outs = (own.at[0], own.at[1], cross.at[0], cross.at[1], far_two, far_six)
+    for k in range(6):
         w_copies[k].wait()
         outs[k][0], outs[k][1] = half_block(w, k, both)
 
@@ -99,27 +99,28 @@
 def early_half(side, order, blocks, landed):
     rows, size = blocks[0].shape[1:]
     owners, _, _, short, width = landed.shape
+    one = VMEM((2, rows, 2 * width), jnp.bfloat16)
     two = VMEM((2, 2, rows, 2 * width), jnp.bfloat16)
     return pl.pallas_call(
         early_kernel,
-        out_shape=[VMEM((size, 4 * width), jnp.bfloat16), two, two]
-        + [VMEM((2, 4, rows, size), jnp.bfloat16)],
-        in_specs=[pl.BlockSpec(memory_space=pltpu.SMEM), DENSE] + [FAR] * 5,
-        out_specs=[DENSE] * 4,
+        out_shape=[VMEM((size, 4 * width), jnp.bfloat16), two, two, one, one]
+        + [VMEM((2, 6, rows, size), jnp.bfloat16)],
+        in_specs=[pl.BlockSpec(memory_space=pltpu.SMEM), DENSE] + [FAR] * 7,
+        out_specs=[DENSE] * 6,
         scratch_shapes=[
             pltpu.VMEM((owners, short, 4 * width), jnp.bfloat16),
-            pltpu.SemaphoreType.DMA((4,)),
+            pltpu.SemaphoreType.DMA((6,)),
             pltpu.SemaphoreType.DMA((4,)),
         ],
         compiler_params=PARAMS,
         cost_estimate=pl.CostEstimate(
-            flops=4 * size * size * 4 * width, bytes_accessed=5 * 2**20, transcendentals=0
+            flops=5 * size * size * 4 * width, bytes_accessed=5 * 2**20, transcendentals=0
         ),
         name="early",
     )(side, *near([order]), *far([landed, *blocks]))
 
 
-def pair_kernel(both_ref, w_ref, v_ref, one_ref, two_ref, w, sems):
+def late_kernel(both_ref, w_ref, v_ref, one_ref, two_ref, w, sems):
     copies = [
         pltpu.make_async_copy(ref, w.at[:, k], sems.at[k]) for k, ref in enumerate((w_ref, v_ref))
     ]
@@ -130,11 +131,11 @@
         out[0], out[1] = half_block(w, k, both_ref[...])
 
 
-def pair_half(both, blocks):
+def late_half(both, blocks):
     rows, size = blocks[0].shape[1:]
     one = VMEM((2, rows, both.shape[1] // 2), jnp.bfloat16)
     return pl.pallas_call(
-        pair_kernel,
+        late_kernel,
         out_shape=[one, one, VMEM((2, 2, rows, size), jnp.bfloat16)],
         in_specs=[DENSE, FAR, DENSE],
         out_specs=[DENSE] * 3,
@@ -143,13 +144,14 @@
         cost_estimate=pl.CostEstimate(
             flops=8 * rows * size * both.shape[1], bytes_accessed=2 * 2**20, transcendentals=0
         ),
+        name="late",
     )(*near([both]), *far(blocks[:1]), *near(blocks[1:]))
 
 
-def tangent_kernel(side_ref, four, first_two, last_two, *refs):
+def tangent_kernel(side_ref, six, two, *refs):
     (own, cross, zn_first, zn_last, far_first, far_last), out_ref = refs[:6], refs[6]
     mixed = refs[7]
-    rows, size = four.shape[2:]
+    rows, size = six.shape[2:]
     owners = out_ref.shape[0]
     wide = size // 2
 
@@ -157,17 +159,15 @@
         return jnp.concatenate([h[part] for part in range(2) for h in (first, last)], axis=0)
 
     zn, distant = stacked(zn_first, zn_last), stacked(far_first, far_last)
-    lefts = (
-        jnp.concatenate([stacked(h.at[0], h.at[1]) for h in (own, cross)], axis=1),
-        jnp.concatenate([zn[:, :rows], distant[:, :rows]], axis=1),
-        jnp.concatenate([zn[:, rows:], distant[:, rows:]], axis=1),
-    )
+    inside = [stacked(h.at[0], h.at[1]) for h in (own, cross)]
+    most = jnp.concatenate(inside + [zn[:, :rows], distant[:, :rows]], axis=1)
+    rest = jnp.concatenate([zn[:, rows:], distant[:, rows:]], axis=1)
     for h in range(2):
         lanes = slice(h * wide, h * wide + wide)
 
         def by(part):
             total = 0.0
-            for left, w in zip(lefts, (four, first_two, last_two)):
+            for left, w in ((most, six), (rest, two)):
                 right = w[part, :, :, lanes].reshape(left.shape[1], wide)
                 total += jnp.dot(left, right, preferred_element_type=jnp.float32)
             return total
@@ -190,7 +190,7 @@
     return pl.pallas_call(
         tangent_kernel,
         out_shape=jax.ShapeDtypeStruct((owners, 2, 8, size), jnp.bfloat16),
-        in_specs=[pl.BlockSpec(memory_space=pltpu.SMEM)] + [DENSE] * 9,
+        in_specs=[pl.BlockSpec(memory_space=pltpu.SMEM)] + [DENSE] * 8,
         out_specs=DENSE,
         scratch_shapes=[pltpu.VMEM((2 * owners, 8, size // 2), jnp.float32)],
         compiler_params=PARAMS,
@@ -226,22 +226,20 @@
 
     across.append(swap(other, ("zn",), 1))
     blocks = [mine, other] + across
-    blocks += [swap(block, ("c",), 1) for block in blocks[:2]]
-    blocks.append(swap(blocks[2], ("c",), 1))
+    blocks += [swap(block, ("c",), 1) for block in blocks[:3]]
     blocks.append(swap(blocks[3], ("c",), 1))
 
-    ready = [blocks[k] for k in (0, 1, 4, 5)]
-    both, own, cross, four = early_half(side, order, ready, landed)
-    zn_first, far_first, first_two = pair_half(both, [blocks[2], blocks[6]])
+    ready = [blocks[k] for k in (0, 1, 4, 5, 2, 6)]
+    both, own, cross, zn_first, far_first, six = early_half(side, order, ready, landed)
     zn_first = swap(zn_first, ("zn",), 1)
     far_first = swap(far_first, ("zn", "c"), 3)
-    cross = swap(cross, ("c",), 1)
-    zn_last, far_last, last_two = pair_half(both, [blocks[3], blocks[7]])
+    zn_last, far_last, two = late_half(both, [blocks[3], blocks[7]])
     zn_last = swap(zn_last, ("zn",), 1)
     far_last = swap(far_last, ("zn", "c"), 3)
+    cross = swap(cross, ("c",), 1)
     halves = [own, cross, zn_first, zn_last, far_first, far_last]
 
-    result = tangent_product(side, (four, first_two, last_two), halves)
+    result = tangent_product(side, (six, two), halves)
     returned = spread(result.reshape(slots, parts * 4, size))
     returned = returned.at[q_owner].get(mode="promise_in_bounds")
     return returned.reshape(slots, parts, 4, size).astype(jnp.float32)

time: 162 us -> 152 us (0.938)
  waiting for transfers between devices: 103 us -> 96.4 us
  Pallas kernels: 14.2 us -> 12.1 us
    ppermute x12, waiting for transfers between devices: 73.9 us -> 66.6 us  [swap(): return lax.ppermute(x, axes, [(i, i ^ mask) for i in range(count)])]
    pallas_call x2 -> x1, Pallas kernels: 6.01 us -> 3.01 us  [late_half(): pl.pallas_call(late_kernel, out_shape=[one, one, VMEM((2, 2, rows, size),...]
  transfers between devices with their start and end apart: 14 -> 14, of which waited for: 7 -> 7; matrix products, arithmetic and copies ran while one was open for 1% -> 1% of each run, Pallas kernels for 7% -> 6%
where the time goes in v3:
time: 152 us; the launch traced here: 151 us
  waiting for transfers between devices  96.4 us (63%)
  starting transfers between devices  34.6 us (23%)
  Pallas kernels  12.1 us (8%)
  local copies, waits for them, and re-layouts  7.29 us (5%)
    ppermute x12, waiting for transfers between devices, swap(): return lax.ppermute(x, axes, [(i, i ^ mask) for i in range(count)])  66.6 us
    all_to_all x2, waiting for transfers between devices, spread(): return lax.all_to_all(x, SPREAD, 0, 0, tiled=True)  29.8 us
    all_to_all x2, starting transfers between devices, spread(): return lax.all_to_all(x, SPREAD, 0, 0, tiled=True)  26.4 us
    ppermute x12, starting transfers between devices, swap(): return lax.ppermute(x, axes, [(i, i ^ mask) for i in range(count)])  8.24 us
    pallas_call x1, Pallas kernels, early_half(): pl.pallas_call(early_kernel, out_shape=[VMEM((size, 4 * width), jnp.bfloa...  5.27 us
    pallas_call x1, Pallas kernels, tangent_product(): pl.pallas_call(tangent_kernel, out_shape=jax.ShapeDtypeStruct((owners, 2,...  3.43 us
  transfers between devices with their start and end apart: 14, of which 7 were waited for; matrix products, arithmetic and copies ran while one was open for 1% of the time, Pallas kernels for 6%

profile of v3, /device:TPU:2, one launch (start us, length us, event | category | flops | bytes accessed | tf_op | source)
XLA Modules:
  0.0 151.5 jit_solution(12972901077453401785)
XLA Ops:
  0.0 0.0 copy-start
  0.0 0.8 select_reduce_fusion
  0.9 0.4 copy-done
  1.2 0.0 copy-start.2
  1.2 1.6 %gather_fusion = bf16[64,2,32,128]{3,2,1,0:T(8,128)(2,1)} fusion(bf16[64,2,32,128]{3,2,1,0:T(8,128)(2,1)S(1)} %copy-done, s32[1024]{0:T(1024)S(1)} %pad_clamp_fusion.1), kind=kCustom, calls=%fused_computation | custom fusion | bytes 2097408 | tf_op jit(solution)/shard_map/gather | solution.py:223
  2.9 0.0 copy-start.3
  2.9 15.0 %all-to-all-start = ((bf16[64,2,32,128]{3,2,1,0:T(8,128)(2,1)}), bf16[64,2,32,128]{3,2,1,0:T(8,128)(2,1)}, u32[]{:S(2)}, u32[]{:S(2)}) async-start(bf16[64,2,32,128]{3,2,1,0:T(8,128)(2,1)} %gather_fusion), calls=%async_computation | async-start | bytes 2097152 | tf_op jit(solution)/shard_map/all_to_all | solution.py:33
  17.9 0.0 copy-done.2
  17.9 2.4 %collective-permute-start = (bf16[2,128,1024]{2,1,0:T(8,128)(2,1)S(1)}, bf16[2,128,1024]{2,1,0:T(8,128)(2,1)}, u32[]{:S(2)}, u32[]{:S(2)}) collective-permute-start(bf16[2,128,1024]{2,1,0:T(8,128)(2,1)S(1)} %dynamic-slice_bitcast_fusion.1), channel_id=1, source_target_pairs={{0,4},{4,0},{1,5},{5,1},{2,6},{6,2},{3,7},{7,3},{8,12},{12,8},{9,1... | collective-permute-start | bytes 1572872 | tf_op jit(solution)/shard_map/ppermute | solution.py:21
  20.4 0.9 dynamic-slice_bitcast_fusion.refs_0_
  21.2 1.0 collective-permute-start.3
  22.3 42.8 %collective-permute-done.refs_1_ = bf16[2,128,1024]{2,1,0:T(8,128)(2,1)} collective-permute-done((bf16[2,128,1024]{2,1,0:T(8,128)(2,1)S(1)}, bf16[2,128,1024]{2,1,0:T(8,128)(2,1)}, u32[]{:S(2)}, u32[]{:S(2)}) %collective-permute-start) | collective-permute-done | bytes 524320 | tf_op jit(solution)/shard_map/ppermute | solution.py:21
  65.1 0.0 collective-permute-start.5
  65.1 0.0 collective-permute-start.1
  65.1 0.0 collective-permute-done.3.refs_4_
  65.1 0.5 collective-permute-start.4
  65.6 0.1 collective-permute-start.2
  65.7 13.1 %collective-permute-done.5.w_ref = bf16[2,128,1024]{2,1,0:T(8,128)(2,1)} collective-permute-done((bf16[2,128,1024]{2,1,0:T(8,128)(2,1)}, bf16[2,128,1024]{2,1,0:T(8,128)(2,1)}, u32[]{:S(2)}, u32[]{:S(2)}) %collective-permute-start.5) | collective-permute-done | bytes 524320 | tf_op jit(solution)/shard_map/ppermute | solution.py:21
  78.8 0.0 collective-permute-start.6
  78.8 0.0 copy-done.3
  78.8 1.0 copy.6.table_ref
  79.8 0.0 copy-start.1
  79.8 1.0 copy-done.1
  80.9 0.4 order.1.order_ref
  81.3 0.0 collective-permute-done.1.refs_2_
  81.3 0.0 collective-permute-done.4.refs_5_
  81.3 0.0 collective-permute-done.2.refs_3_
  81.3 0.0 all-to-all-done
  81.3 5.3 %early.1 = (bf16[1024,512]{1,0:T(8,128)(2,1)S(1)}, bf16[2,2,128,256]{3,2,1,0:T(8,128)(2,1)S(1)}, bf16[2,2,128,256]{3,2,1,0:T(8,128)(2,1)S(1)}, bf16[2,128,256]{2...) custom-call(s32[1]{0:T(128)} %bitcast.side_ref, ...), custom_call_target="tpu_custom_call" | custom-call | flops 2684354560 | bytes 5242880 | tf_op jit(solution)/shard_map/early/pallas_call | solution.py:104
  86.6 0.6 collective-permute-start.7
  87.2 0.0 collective-permute-done.6.v_ref
  87.2 3.0 %late.1 = (bf16[2,128,256]{2,1,0:T(8,128)(2,1)S(1)}, bf16[2,128,256]{2,1,0:T(8,128)(2,1)S(1)}, bf16[2,2,128,1024]{3,2,1,0:T(8,128)(2,1)S(1)}) custom-call(bf16[1024,512]{1,0:T(8,128)(2,1)S(1)} %get-tuple-element.17.both_ref, bf16[2,128,1024]{2,1,0:T(8,128)(2,1)} %collective-permute-done.5.w_ref, bf16[2,128,1024]{2,1,0:T(8,128)(2,1)} %collective-permute-done.6.v_ref), custom_call_target="tpu_custom_call" | custom-call | flops 536870912 | bytes 2097152 | tf_op jit(solution)/shard_map/late/pallas_call | solution.py:137
  90.2 0.1 collective-permute-start.11
  90.3 1.6 %collective-permute-start.9 = (bf16[2,128,256]{2,1,0:T(8,128)(2,1)S(1)}, bf16[2,128,256]{2,1,0:T(8,128)(2,1)S(1)}, u32[]{:S(2)}, u32[]{:S(2)}) collective-permute-start(bf16[2,128,256]{2,1,0:T(8,128)(2,1)S(1)} %get-tuple-element.22), channel_id=1, source_target_pairs={{0,2},{2,0},{1,3},{3,1},{4,6},{6,4},{5,7},{7,5},{8,10},{10,8},{9,1... | collective-permute-start | bytes 393224 | tf_op jit(solution)/shard_map/ppermute | solution.py:21
  92.0 0.1 collective-permute-start.10
  92.1 1.7 %collective-permute-start.8 = (bf16[2,128,256]{2,1,0:T(8,128)(2,1)S(1)}, bf16[2,128,256]{2,1,0:T(8,128)(2,1)S(1)}, u32[]{:S(2)}, u32[]{:S(2)}) collective-permute-start(bf16[2,128,256]{2,1,0:T(8,128)(2,1)S(1)} %get-tuple-element.21), channel_id=1, source_target_pairs={{0,2},{2,0},{1,3},{3,1},{4,6},{6,4},{5,7},{7,5},{8,10},{10,8},{9,1... | collective-permute-start | bytes 393224 | tf_op jit(solution)/shard_map/ppermute | solution.py:21
  93.8 2.1 %collective-permute-done.11.refs_5_ = bf16[2,128,256]{2,1,0:T(8,128)(2,1)S(1)} collective-permute-done((bf16[2,128,256]{2,1,0:T(8,128)(2,1)S(1)}, bf16[2,128,256]{2,1,0:T(8,128)(2,1)S(1)}, u32[]{:S(2)}, u32[]{:S(2)}) %collective-permute-start.11) | collective-permute-done | bytes 131104 | tf_op jit(solution)/shard_map/ppermute | solution.py:21
  95.9 3.2 %collective-permute-done.9.refs_3_ = bf16[2,128,256]{2,1,0:T(8,128)(2,1)S(1)} collective-permute-done((bf16[2,128,256]{2,1,0:T(8,128)(2,1)S(1)}, bf16[2,128,256]{2,1,0:T(8,128)(2,1)S(1)}, u32[]{:S(2)}, u32[]{:S(2)}) %collective-permute-start.9) | collective-permute-done | bytes 131104 | tf_op jit(solution)/shard_map/ppermute | solution.py:21
  99.1 2.4 %collective-permute-done.10.refs_4_ = bf16[2,128,256]{2,1,0:T(8,128)(2,1)S(1)} collective-permute-done((bf16[2,128,256]{2,1,0:T(8,128)(2,1)S(1)}, bf16[2,128,256]{2,1,0:T(8,128)(2,1)S(1)}, u32[]{:S(2)}, u32[]{:S(2)}) %collective-permute-start.10) | collective-permute-done | bytes 131104 | tf_op jit(solution)/shard_map/ppermute | solution.py:21
  101.5 3.0 %collective-permute-done.8.refs_2_ = bf16[2,128,256]{2,1,0:T(8,128)(2,1)S(1)} collective-permute-done((bf16[2,128,256]{2,1,0:T(8,128)(2,1)S(1)}, bf16[2,128,256]{2,1,0:T(8,128)(2,1)S(1)}, u32[]{:S(2)}, u32[]{:S(2)}) %collective-permute-start.8) | collective-permute-done | bytes 131104 | tf_op jit(solution)/shard_map/ppermute | solution.py:21
  104.5 0.0 collective-permute-done.7.refs_1_
  104.5 3.4 %tangent.1 = bf16[32,2,8,1024]{3,2,1,0:T(8,128)(2,1)} custom-call(s32[1]{0:T(128)} %bitcast.side_ref, bf16[2,6,128,1024]{3,2,1,0:T(8,128)(2,1)S(1)} %get-tuple-element.16.six, bf16[2,2,128,1024]{3,2,1,0:T(8,128)(2,1)S(1)} %get-tuple-element.18.two, bf16[2,2,128,256]{3,2,1,0:T(8,128)(2,1)S(1)} %get-tuple-element.19.refs_0_, ...), custom_call_target="tpu_custom_call" | custom-call | flops 2147483648 | bytes 3145728 | tf_op jit(solution)/shard_map/tangent/pallas_call | solution.py:190
  108.0 0.0 copy-start.4
  108.0 11.4 %all-to-all-start.1 = ((bf16[64,8,1024]{2,1,0:T(8,128)(2,1)}), bf16[64,8,1024]{2,1,0:T(8,128)(2,1)S(1)}, u32[]{:S(2)}, u32[]{:S(2)}) async-start(bf16[64,8,1024]{2,1,0:T(8,128)(2,1)} %bitcast.7), calls=%async_computation.1 | async-start | bytes 2097152 | tf_op jit(solution)/shard_map/all_to_all | solution.py:33
  119.4 0.0 copy-done.4
  119.4 29.8 %all-to-all-done.1 = bf16[64,8,1024]{2,1,0:T(8,128)(2,1)S(1)} async-done(((bf16[64,8,1024]{2,1,0:T(8,128)(2,1)}), bf16[64,8,1024]{2,1,0:T(8,128)(2,1)S(1)}, u32[]{:S(2)}, u32[]{:S(2)}) %all-to-all-start.1) | async-done | bytes 1048608 | tf_op jit(solution)/shard_map/all_to_all | solution.py:33
  149.2 0.6 gather_fusion.1
  149.8 1.7 %reshape.26 = f32[64,2,4,1024]{3,2,1,0:T(4,128)} reshape(bf16[64,8,1024]{2,1,0:T(8,128)(2,1)S(1)} %gather_fusion.1) | data formatting | bytes 3145728 | tf_op jit(solution)/shard_map/convert_element_type | solution.py:245
  (6 shorter events, 0.1 us)
Async XLA Ops:
  0.0 1.2 copy-start
  1.2 16.6 %copy-start.2 = (bf16[2,2,128,1024]{3,2,1,0:T(8,128)(2,1)S(1)}, bf16[2,2,128,1024]{3,2,1,0:T(8,128)(2,1)}, u32[]{:S(2)}) copy-start(bf16[2,2,128,1024]{3,2,1,0:T(8,128)(2,1)} %param.4) | copy-start | bytes 3145732
  2.9 75.9 %copy-start.3 = (s32[2,1024]{1,0:T(2,128)S(1)}, s32[2,1024]{1,0:T(2,128)}, u32[]{:S(2)}) copy-start(s32[2,1024]{1,0:T(2,128)} %param.7) | copy-start | bytes 24580
  2.9 78.4 %all-to-all-start = ((bf16[64,2,32,128]{3,2,1,0:T(8,128)(2,1)}), bf16[64,2,32,128]{3,2,1,0:T(8,128)(2,1)}, u32[]{:S(2)}, u32[]{:S(2)}) async-start(bf16[64,2,32,128]{3,2,1,0:T(8,128)(2,1)} %gather_fusion), calls=%async_computation | async-start | bytes 2097152 | tf_op jit(solution)/shard_map/all_to_all | solution.py:33
  17.9 47.1 %collective-permute-start = (bf16[2,128,1024]{2,1,0:T(8,128)(2,1)S(1)}, bf16[2,128,1024]{2,1,0:T(8,128)(2,1)}, u32[]{:S(2)}, u32[]{:S(2)}) collective-permute-start(bf16[2,128,1024]{2,1,0:T(8,128)(2,1)S(1)} %dynamic-slice_bitcast_fusion.1), channel_id=1, source_target_pairs={{0,4},{4,0},{1,5},{5,1},{2,6},{6,2},{3,7},{7,3},{8,12},{12,8},{9,1... | collective-permute-start | bytes 1572872 | tf_op jit(solution)/shard_map/ppermute | solution.py:21
  21.2 43.8 %collective-permute-start.3 = (bf16[2,128,1024]{2,1,0:T(8,128)(2,1)}, bf16[2,128,1024]{2,1,0:T(8,128)(2,1)}, u32[]{:S(2)}, u32[]{:S(2)}) collective-permute-start(bf16[2,128,1024]{2,1,0:T(8,128)(2,1)} %dynamic-slice_bitcast_fusion.refs_0_), channel_id=1, source_target_pairs={{0,2},{2,0},{1,3},{3,1},{4,6},{6,4},{5,7},{7,5},{8,10},{10,8},{9,1... | collective-permute-start | bytes 1572872 | tf_op jit(solution)/shard_map/ppermute | solution.py:21
  65.1 13.7 %collective-permute-start.5 = (bf16[2,128,1024]{2,1,0:T(8,128)(2,1)}, bf16[2,128,1024]{2,1,0:T(8,128)(2,1)}, u32[]{:S(2)}, u32[]{:S(2)}) collective-permute-start(bf16[2,128,1024]{2,1,0:T(8,128)(2,1)} %collective-permute-done.refs_1_), channel_id=1, source_target_pairs={{0,2},{2,0},{1,3},{3,1},{4,6},{6,4},{5,7},{7,5},{8,10},{10,8},{9,1... | collective-permute-start | bytes 1572872 | tf_op jit(solution)/shard_map/ppermute | solution.py:21
  65.1 16.2 %collective-permute-start.1 = (bf16[2,128,1024]{2,1,0:T(8,128)(2,1)}, bf16[2,128,1024]{2,1,0:T(8,128)(2,1)}, u32[]{:S(2)}, u32[]{:S(2)}) collective-permute-start(bf16[2,128,1024]{2,1,0:T(8,128)(2,1)} %dynamic-slice_bitcast_fusion.refs_0_), channel_id=1, source_target_pairs={{0,1},{1,0},{2,3},{3,2},{4,5},{5,4},{6,7},{7,6},{8,9},{9,8},{10,11... | collective-permute-start | bytes 1572872 | tf_op jit(solution)/shard_map/ppermute | solution.py:21
  65.1 16.2 %collective-permute-start.4 = (bf16[2,128,1024]{2,1,0:T(8,128)(2,1)}, bf16[2,128,1024]{2,1,0:T(8,128)(2,1)}, u32[]{:S(2)}, u32[]{:S(2)}) collective-permute-start(bf16[2,128,1024]{2,1,0:T(8,128)(2,1)} %collective-permute-done.3.refs_4_), channel_id=1, source_target_pairs={{0,1},{1,0},{2,3},{3,2},{4,5},{5,4},{6,7},{7,6},{8,9},{9,8},{10,11... | collective-permute-start | bytes 1572872 | tf_op jit(solution)/shard_map/ppermute | solution.py:21
  65.6 15.7 %collective-permute-start.2 = (bf16[2,128,1024]{2,1,0:T(8,128)(2,1)}, bf16[2,128,1024]{2,1,0:T(8,128)(2,1)}, u32[]{:S(2)}, u32[]{:S(2)}) collective-permute-start(bf16[2,128,1024]{2,1,0:T(8,128)(2,1)} %collective-permute-done.refs_1_), channel_id=1, source_target_pairs={{0,1},{1,0},{2,3},{3,2},{4,5},{5,4},{6,7},{7,6},{8,9},{9,8},{10,11... | collective-permute-start | bytes 1572872 | tf_op jit(solution)/shard_map/ppermute | solution.py:21
  78.8 8.4 %collective-permute-start.6 = (bf16[2,128,1024]{2,1,0:T(8,128)(2,1)}, bf16[2,128,1024]{2,1,0:T(8,128)(2,1)}, u32[]{:S(2)}, u32[]{:S(2)}) collective-permute-start(bf16[2,128,1024]{2,1,0:T(8,128)(2,1)} %collective-permute-done.5.w_ref), channel_id=1, source_target_pairs={{0,1},{1,0},{2,3},{3,2},{4,5},{5,4},{6,7},{7,6},{8,9},{9,8},{10,11... | collective-permute-start | bytes 1572872 | tf_op jit(solution)/shard_map/ppermute | solution.py:21
  79.8 1.0 copy-start.1
  86.6 17.9 %collective-permute-start.7 = (bf16[2,2,128,256]{3,2,1,0:T(8,128)(2,1)S(1)}, bf16[2,2,128,256]{3,2,1,0:T(8,128)(2,1)S(1)}, u32[]{:S(2)}, u32[]{:S(2)}) collective-permute-start(bf16[2,2,128,256]{3,2,1,0:T(8,128)(2,1)S(1)} %get-tuple-element.20), channel_id=1, source_target_pairs={{0,1},{1,0},{2,3},{3,2},{4,5},{5,4},{6,7},{7,6},{8,9},{9,8},{10,11... | collective-permute-start | bytes 786440 | tf_op jit(solution)/shard_map/ppermute | solution.py:21
  90.2 5.7 %collective-permute-start.11 = (bf16[2,128,256]{2,1,0:T(8,128)(2,1)S(1)}, bf16[2,128,256]{2,1,0:T(8,128)(2,1)S(1)}, u32[]{:S(2)}, u32[]{:S(2)}) collective-permute-start(bf16[2,128,256]{2,1,0:T(8,128)(2,1)S(1)} %get-tuple-element.24), channel_id=1, source_target_pairs={{0,3},{1,2},{2,1},{3,0},{4,7},{5,6},{6,5},{7,4},{8,11},{9,10},{10,... | collective-permute-start | bytes 393224 | tf_op jit(solution)/shard_map/ppermute | solution.py:21
  90.3 8.8 %collective-permute-start.9 = (bf16[2,128,256]{2,1,0:T(8,128)(2,1)S(1)}, bf16[2,128,256]{2,1,0:T(8,128)(2,1)S(1)}, u32[]{:S(2)}, u32[]{:S(2)}) collective-permute-start(bf16[2,128,256]{2,1,0:T(8,128)(2,1)S(1)} %get-tuple-element.22), channel_id=1, source_target_pairs={{0,2},{2,0},{1,3},{3,1},{4,6},{6,4},{5,7},{7,5},{8,10},{10,8},{9,1... | collective-permute-start | bytes 393224 | tf_op jit(solution)/shard_map/ppermute | solution.py:21
  92.0 9.6 %collective-permute-start.10 = (bf16[2,128,256]{2,1,0:T(8,128)(2,1)S(1)}, bf16[2,128,256]{2,1,0:T(8,128)(2,1)S(1)}, u32[]{:S(2)}, u32[]{:S(2)}) collective-permute-start(bf16[2,128,256]{2,1,0:T(8,128)(2,1)S(1)} %get-tuple-element.23), channel_id=1, source_target_pairs={{0,3},{1,2},{2,1},{3,0},{4,7},{5,6},{6,5},{7,4},{8,11},{9,10},{10,... | collective-permute-start | bytes 393224 | tf_op jit(solution)/shard_map/ppermute | solution.py:21
  92.1 12.5 %collective-permute-start.8 = (bf16[2,128,256]{2,1,0:T(8,128)(2,1)S(1)}, bf16[2,128,256]{2,1,0:T(8,128)(2,1)S(1)}, u32[]{:S(2)}, u32[]{:S(2)}) collective-permute-start(bf16[2,128,256]{2,1,0:T(8,128)(2,1)S(1)} %get-tuple-element.21), channel_id=1, source_target_pairs={{0,2},{2,0},{1,3},{3,1},{4,6},{6,4},{5,7},{7,5},{8,10},{10,8},{9,1... | collective-permute-start | bytes 393224 | tf_op jit(solution)/shard_map/ppermute | solution.py:21
  108.0 11.4 %copy-start.4 = (s32[64]{0:T(128)S(1)}, s32[64]{0:T(128)}, u32[]{:S(2)}) copy-start(s32[64]{0:T(128)} %param.6) | copy-start | bytes 772
  108.0 41.2 %all-to-all-start.1 = ((bf16[64,8,1024]{2,1,0:T(8,128)(2,1)}), bf16[64,8,1024]{2,1,0:T(8,128)(2,1)S(1)}, u32[]{:S(2)}, u32[]{:S(2)}) async-start(bf16[64,8,1024]{2,1,0:T(8,128)(2,1)} %bitcast.7), calls=%async_computation.1 | async-start | bytes 2097152 | tf_op jit(solution)/shard_map/all_to_all | solution.py:33

commit v4 on v2

--- a/solution.py
+++ b/solution.py
@@ -64,8 +64,8 @@
 
 
 def early_kernel(side_ref, order_ref, landed_ref, *refs):
-    w_refs, both_ref, own, cross, w = refs[:4], *refs[4:8]
-    chi, w_sems, chi_sems = refs[8:]
+    w_refs, both_ref, one, two, w = refs[:2], *refs[2:6]
+    chi, w_sems, chi_sems = refs[6:]
     width = landed_ref.shape[-1]
     side = side_ref[0]
     chi_copies, w_copies = [], []
@@ -79,7 +79,7 @@
                     chi_sems.at[at],
                 )
             )
-    for k in range(4):
+    for k in range(2):
         w_copies.append(pltpu.make_async_copy(w_refs[k], w.at[:, k], w_sems.at[k]))
     for copy in chi_copies + w_copies:
         copy.start()
@@ -90,8 +90,8 @@
     both = jnp.dot(order_ref[...], both, preferred_element_type=jnp.float32)
     both = both.astype(jnp.bfloat16)
     both_ref[...] = both
-    outs = (own.at[0], own.at[1], cross.at[0], cross.at[1])
-    for k in range(4):
+    outs = (one, two)
+    for k in range(2):
         w_copies[k].wait()
         outs[k][0], outs[k][1] = half_block(w, k, both)
 
@@ -99,21 +99,21 @@
 def early_half(side, order, blocks, landed):
     rows, size = blocks[0].shape[1:]
     owners, _, _, short, width = landed.shape
-    two = VMEM((2, 2, rows, 2 * width), jnp.bfloat16)
+    one = VMEM((2, rows, 2 * width), jnp.bfloat16)
     return pl.pallas_call(
         early_kernel,
-        out_shape=[VMEM((size, 4 * width), jnp.bfloat16), two, two]
-        + [VMEM((2, 4, rows, size), jnp.bfloat16)],
-        in_specs=[pl.BlockSpec(memory_space=pltpu.SMEM), DENSE] + [FAR] * 5,
+        out_shape=[VMEM((size, 4 * width), jnp.bfloat16), one, one]
+        + [VMEM((2, 2, rows, size), jnp.bfloat16)],
+        in_specs=[pl.BlockSpec(memory_space=pltpu.SMEM), DENSE] + [FAR] * 3,
         out_specs=[DENSE] * 4,
         scratch_shapes=[
             pltpu.VMEM((owners, short, 4 * width), jnp.bfloat16),
-            pltpu.SemaphoreType.DMA((4,)),
+            pltpu.SemaphoreType.DMA((2,)),
             pltpu.SemaphoreType.DMA((4,)),
         ],
         compiler_params=PARAMS,
         cost_estimate=pl.CostEstimate(
-            flops=4 * size * size * 4 * width, bytes_accessed=5 * 2**20, transcendentals=0
+            flops=3 * size * size * 4 * width, bytes_accessed=5 * 2**20, transcendentals=0
         ),
         name="early",
     )(side, *near([order]), *far([landed, *blocks]))
@@ -144,6 +144,35 @@
             flops=8 * rows * size * both.shape[1], bytes_accessed=2 * 2**20, transcendentals=0
         ),
     )(*near([both]), *far(blocks[:1]), *near(blocks[1:]))
+
+
+def inside_kernel(both_ref, *refs):
+    w_refs, own, cross, w, sems = refs[:4], *refs[4:8]
+    copies = [
+        pltpu.make_async_copy(ref, w.at[:, k], sems.at[k]) for k, ref in enumerate(w_refs)
+    ]
+    for copy in copies:
+        copy.start()
+    for k, out in enumerate((own.at[0], own.at[1], cross.at[0], cross.at[1])):
+        copies[k].wait()
+        out[0], out[1] = half_block(w, k, both_ref[...])
+
+
+def inside_half(both, blocks):
+    rows, size = blocks[0].shape[1:]
+    two = VMEM((2, 2, rows, both.shape[1] // 2), jnp.bfloat16)
+    return pl.pallas_call(
+        inside_kernel,
+        out_shape=[two, two, VMEM((2, 4, rows, size), jnp.bfloat16)],
+        in_specs=[DENSE] + [FAR] * 4,
+        out_specs=[DENSE] * 3,
+        scratch_shapes=[pltpu.SemaphoreType.DMA((4,))],
+        compiler_params=PARAMS,
+        cost_estimate=pl.CostEstimate(
+            flops=16 * rows * size * both.shape[1], bytes_accessed=4 * 2**20, transcendentals=0
+        ),
+        name="inside",
+    )(*near([both]), *far(blocks))
 
 
 def tangent_kernel(side_ref, four, first_two, last_two, *refs):
@@ -226,19 +255,17 @@
 
     across.append(swap(other, ("zn",), 1))
     blocks = [mine, other] + across
-    blocks += [swap(block, ("c",), 1) for block in blocks[:2]]
-    blocks.append(swap(blocks[2], ("c",), 1))
+    blocks += [swap(block, ("c",), 1) for block in blocks[:3]]
     blocks.append(swap(blocks[3], ("c",), 1))
 
-    ready = [blocks[k] for k in (0, 1, 4, 5)]
-    both, own, cross, four = early_half(side, order, ready, landed)
-    zn_first, far_first, first_two = pair_half(both, [blocks[2], blocks[6]])
+    both, zn_first, far_first, first_two = early_half(side, order, [blocks[2], blocks[6]], landed)
     zn_first = swap(zn_first, ("zn",), 1)
     far_first = swap(far_first, ("zn", "c"), 3)
-    cross = swap(cross, ("c",), 1)
     zn_last, far_last, last_two = pair_half(both, [blocks[3], blocks[7]])
     zn_last = swap(zn_last, ("zn",), 1)
     far_last = swap(far_last, ("zn", "c"), 3)
+    own, cross, four = inside_half(both, [blocks[k] for k in (0, 1, 4, 5)])
+    cross = swap(cross, ("c",), 1)
     halves = [own, cross, zn_first, zn_last, far_first, far_last]
 
     result = tangent_product(side, (four, first_two, last_two), halves)

time: 162 us -> 150 us (0.926)
  waiting for transfers between devices: 103 us -> 91.4 us
    ppermute x12, waiting for transfers between devices: 73.9 us -> 62.8 us  [swap(): return lax.ppermute(x, axes, [(i, i ^ mask) for i in range(count)])]
    pallas_call x2 -> x1, Pallas kernels: 6.01 us -> 3 us  [pair_half(): pl.pallas_call(pair_kernel, out_shape=[one, one, VMEM((2, 2, rows, size),...]
    pallas_call x0 -> x1, Pallas kernels: none -> 2.89 us  [inside_half(): pl.pallas_call(inside_kernel, out_shape=[two, two, VMEM((2, 4, rows, size...]
  transfers between devices with their start and end apart: 14 -> 14, of which waited for: 7 -> 6; matrix products, arithmetic and copies ran while one was open for 1% -> 1% of each run, Pallas kernels for 7% -> 7%
where the time goes in v4:
time: 150 us; the launch traced here: 148 us
  waiting for transfers between devices  91.4 us (61%)
  starting transfers between devices  34.9 us (23%)
  Pallas kernels  13.2 us (9%)
  local copies, waits for them, and re-layouts  7.29 us (5%)
    ppermute x12, waiting for transfers between devices, swap(): return lax.ppermute(x, axes, [(i, i ^ mask) for i in range(count)])  62.8 us
    all_to_all x2, waiting for transfers between devices, spread(): return lax.all_to_all(x, SPREAD, 0, 0, tiled=True)  28.6 us
    all_to_all x2, starting transfers between devices, spread(): return lax.all_to_all(x, SPREAD, 0, 0, tiled=True)  26.4 us
    ppermute x12, starting transfers between devices, swap(): return lax.ppermute(x, axes, [(i, i ^ mask) for i in range(count)])  8.54 us
    pallas_call x1, Pallas kernels, tangent_product(): pl.pallas_call(tangent_kernel, out_shape=jax.ShapeDtypeStruct((owners, 2,...  3.45 us
    pallas_call x1, Pallas kernels, early_half(): pl.pallas_call(early_kernel, out_shape=[VMEM((size, 4 * width), jnp.bfloa...  3.41 us
    pallas_call x1, Pallas kernels, pair_half(): pl.pallas_call(pair_kernel, out_shape=[one, one, VMEM((2, 2, rows, size),...  3 us
  transfers between devices with their start and end apart: 14, of which 6 were waited for; matrix products, arithmetic and copies ran while one was open for 1% of the time, Pallas kernels for 7%

profile of v4, /device:TPU:2, one launch (start us, length us, event | category | flops | bytes accessed | tf_op | source)
XLA Modules:
  0.0 147.8 jit_solution(11403093341924329050)
XLA Ops:
  0.0 0.0 copy-start
  0.0 0.8 select_reduce_fusion
  0.9 0.4 copy-done
  1.2 0.0 copy-start.2
  1.2 1.6 %gather_fusion = bf16[64,2,32,128]{3,2,1,0:T(8,128)(2,1)} fusion(bf16[64,2,32,128]{3,2,1,0:T(8,128)(2,1)S(1)} %copy-done, s32[1024]{0:T(1024)S(1)} %pad_clamp_fusion.1), kind=kCustom, calls=%fused_computation | custom fusion | bytes 2097408 | tf_op jit(solution)/shard_map/gather | solution.py:252
  2.9 0.0 copy-start.3
  2.9 15.0 %all-to-all-start = ((bf16[64,2,32,128]{3,2,1,0:T(8,128)(2,1)}), bf16[64,2,32,128]{3,2,1,0:T(8,128)(2,1)}, u32[]{:S(2)}, u32[]{:S(2)}) async-start(bf16[64,2,32,128]{3,2,1,0:T(8,128)(2,1)} %gather_fusion), calls=%async_computation | async-start | bytes 2097152 | tf_op jit(solution)/shard_map/all_to_all | solution.py:33
  17.9 0.0 copy-done.2
  17.9 2.4 %collective-permute-start.2 = (bf16[2,128,1024]{2,1,0:T(8,128)(2,1)S(1)}, bf16[2,128,1024]{2,1,0:T(8,128)(2,1)}, u32[]{:S(2)}, u32[]{:S(2)}) collective-permute-start(bf16[2,128,1024]{2,1,0:T(8,128)(2,1)S(1)} %dynamic-slice_bitcast_fusion.1), channel_id=1, source_target_pairs={{0,4},{4,0},{1,5},{5,1},{2,6},{6,2},{3,7},{7,3},{8,12},{12,8},{9,1... | collective-permute-start | bytes 1572872 | tf_op jit(solution)/shard_map/ppermute | solution.py:21
  20.4 0.9 dynamic-slice_bitcast_fusion.refs_0_
  21.2 1.0 collective-permute-start
  22.3 42.8 %collective-permute-done.2.refs_1_ = bf16[2,128,1024]{2,1,0:T(8,128)(2,1)} collective-permute-done((bf16[2,128,1024]{2,1,0:T(8,128)(2,1)S(1)}, bf16[2,128,1024]{2,1,0:T(8,128)(2,1)}, u32[]{:S(2)}, u32[]{:S(2)}) %collective-permute-start.2) | collective-permute-done | bytes 524320 | tf_op jit(solution)/shard_map/ppermute | solution.py:21
  65.1 0.0 collective-permute-start.5
  65.1 0.0 collective-permute-done.refs_0_
  65.1 0.0 collective-permute-start.1
  65.1 0.5 collective-permute-start.3
  65.6 0.1 collective-permute-start.4
  65.7 13.1 %collective-permute-done.5.w_ref = bf16[2,128,1024]{2,1,0:T(8,128)(2,1)} collective-permute-done((bf16[2,128,1024]{2,1,0:T(8,128)(2,1)}, bf16[2,128,1024]{2,1,0:T(8,128)(2,1)}, u32[]{:S(2)}, u32[]{:S(2)}) %collective-permute-start.5) | collective-permute-done | bytes 524320 | tf_op jit(solution)/shard_map/ppermute | solution.py:21
  78.8 0.0 collective-permute-start.6
  78.8 0.0 copy-done.3
  78.8 1.0 copy.6.table_ref
  79.8 0.0 copy-start.1
  79.8 1.0 copy-done.1
  80.9 0.4 order.1.order_ref
  81.3 0.0 collective-permute-done.1.refs_1_
  81.3 0.0 all-to-all-done
  81.3 3.4 %early.1 = (bf16[1024,512]{1,0:T(8,128)(2,1)S(1)}, bf16[2,128,256]{2,1,0:T(8,128)(2,1)S(1)}, bf16[2,128,256]{2,1,0:T(8,128)(2,1)S(1)}, bf16[2,2,128,1024]{3,2,1,0:T(8,128)(2,1)S(1)}) custom-call(s32[1]{0:T(128)} %bitcast.side_ref, bf16[1024,1024]{1,0:T(8,128)(2,1)S(1)} %order.1.order_ref, bf16[32,2,2,32,128]{4,3,2,1,0:T(8,128)(2,1)} %bitcast.4.landed_ref, ...), custom_call_target="tpu_custom_call" | custom-call | flops 1610612736 | bytes 5242880 | tf_op jit(solution)/shard_map/early/pallas_call | solution.py:103
  84.7 0.0 collective-permute-done.3.refs_2_
  84.7 0.0 collective-permute-done.4.refs_3_
  84.7 2.9 %inside.1 = (bf16[2,2,128,256]{3,2,1,0:T(8,128)(2,1)S(1)}, bf16[2,2,128,256]{3,2,1,0:T(8,128)(2,1)S(1)}, bf16[2,4,128,1024]{3,2,1,0:T(8,128)(2,1)S(1)}) custom-call(bf16[1024,512]{1,0:T(8,128)(2,1)S(1)} %get-tuple-element.17.both_ref, bf16[2,128,1024]{2,1,0:T(8,128)(2,1)} %dynamic-slice_bitcast_fusion.refs_0_, ...), custom_call_target="tpu_custom_call" | custom-call | flops 1073741824 | bytes 4194304 | tf_op jit(solution)/shard_map/inside/pallas_call | solution.py:164
  87.6 0.6 collective-permute-start.7
  88.2 0.3 collective-permute-start.8
  88.5 0.0 collective-permute-done.6.v_ref
  88.5 3.0 %shard_map.46 = (bf16[2,128,256]{2,1,0:T(8,128)(2,1)S(1)}, bf16[2,128,256]{2,1,0:T(8,128)(2,1)S(1)}, bf16[2,2,128,1024]{3,2,1,0:T(8,128)(2,1)S(1)}) custom-call(bf16[1024,512]{1,0:T(8,128)(2,1)S(1)} %get-tuple-element.17.both_ref, bf16[2,128,1024]{2,1,0:T(8,128)(2,1)} %collective-permute-done.5.w_ref, bf16[2,128,1024]{2,1,0:T(8,128)(2,1)} %collective-permute-done.6.v_ref), custom_call_target="tpu_custom_call" | custom-call | flops 536870912 | bytes 2097152 | tf_op jit(solution)/shard_map/pallas_call | solution.py:136
  91.5 1.8 %collective-permute-start.9 = (bf16[2,128,256]{2,1,0:T(8,128)(2,1)S(1)}, bf16[2,128,256]{2,1,0:T(8,128)(2,1)S(1)}, u32[]{:S(2)}, u32[]{:S(2)}) collective-permute-start(bf16[2,128,256]{2,1,0:T(8,128)(2,1)S(1)} %get-tuple-element.24), channel_id=1, source_target_pairs={{0,2},{2,0},{1,3},{3,1},{4,6},{6,4},{5,7},{7,5},{8,10},{10,8},{9,1... | collective-permute-start | bytes 393224 | tf_op jit(solution)/shard_map/ppermute | solution.py:21
  93.4 0.0 collective-permute-start.10
  93.4 1.7 %collective-permute-start.11 = (bf16[2,128,256]{2,1,0:T(8,128)(2,1)S(1)}, bf16[2,128,256]{2,1,0:T(8,128)(2,1)S(1)}, u32[]{:S(2)}, u32[]{:S(2)}) collective-permute-start(bf16[2,128,256]{2,1,0:T(8,128)(2,1)S(1)} %get-tuple-element.26), channel_id=1, source_target_pairs={{0,3},{1,2},{2,1},{3,0},{4,7},{5,6},{6,5},{7,4},{8,11},{9,10},{10,... | collective-permute-start | bytes 393224 | tf_op jit(solution)/shard_map/ppermute | solution.py:21
  95.1 0.0 collective-permute-done.8.refs_2_
  95.1 2.3 %collective-permute-done.9.refs_3_ = bf16[2,128,256]{2,1,0:T(8,128)(2,1)S(1)} collective-permute-done((bf16[2,128,256]{2,1,0:T(8,128)(2,1)S(1)}, bf16[2,128,256]{2,1,0:T(8,128)(2,1)S(1)}, u32[]{:S(2)}, u32[]{:S(2)}) %collective-permute-start.9) | collective-permute-done | bytes 131104 | tf_op jit(solution)/shard_map/ppermute | solution.py:21
  97.4 2.7 %collective-permute-done.10.refs_4_ = bf16[2,128,256]{2,1,0:T(8,128)(2,1)S(1)} collective-permute-done((bf16[2,128,256]{2,1,0:T(8,128)(2,1)S(1)}, bf16[2,128,256]{2,1,0:T(8,128)(2,1)S(1)}, u32[]{:S(2)}, u32[]{:S(2)}) %collective-permute-start.10) | collective-permute-done | bytes 131104 | tf_op jit(solution)/shard_map/ppermute | solution.py:21
  100.1 1.9 %collective-permute-done.11.refs_5_ = bf16[2,128,256]{2,1,0:T(8,128)(2,1)S(1)} collective-permute-done((bf16[2,128,256]{2,1,0:T(8,128)(2,1)S(1)}, bf16[2,128,256]{2,1,0:T(8,128)(2,1)S(1)}, u32[]{:S(2)}, u32[]{:S(2)}) %collective-permute-start.11) | collective-permute-done | bytes 131104 | tf_op jit(solution)/shard_map/ppermute | solution.py:21
  102.0 0.0 collective-permute-done.7.refs_1_
  102.0 3.4 %tangent.1 = bf16[32,2,8,1024]{3,2,1,0:T(8,128)(2,1)} custom-call(s32[1]{0:T(128)} %bitcast.side_ref, bf16[2,4,128,1024]{3,2,1,0:T(8,128)(2,1)S(1)} %get-tuple-element.18.four, bf16[2,2,128,1024]{3,2,1,0:T(8,128)(2,1)S(1)} %get-tuple-element.19.first_two, bf16[2,2,128,1024]{3,2,1,0:T(8,128)(2,1)S(1)} %get-tuple-element.20.last_two, ...), custom_call_target="tpu_custom_call" | custom-call | flops 2147483648 | bytes 3145728 | tf_op jit(solution)/shard_map/tangent/pallas_call | solution.py:219
  105.4 11.4 %all-to-all-start.1 = ((bf16[64,8,1024]{2,1,0:T(8,128)(2,1)}), bf16[64,8,1024]{2,1,0:T(8,128)(2,1)S(1)}, u32[]{:S(2)}, u32[]{:S(2)}) async-start(bf16[64,8,1024]{2,1,0:T(8,128)(2,1)} %bitcast.7), calls=%async_computation.1 | async-start | bytes 2097152 | tf_op jit(solution)/shard_map/all_to_all | solution.py:33
  116.9 0.0 copy-done.4
  116.9 28.6 %all-to-all-done.1 = bf16[64,8,1024]{2,1,0:T(8,128)(2,1)S(1)} async-done(((bf16[64,8,1024]{2,1,0:T(8,128)(2,1)}), bf16[64,8,1024]{2,1,0:T(8,128)(2,1)S(1)}, u32[]{:S(2)}, u32[]{:S(2)}) %all-to-all-start.1) | async-done | bytes 1048608 | tf_op jit(solution)/shard_map/all_to_all | solution.py:33
  145.5 0.6 gather_fusion.1
  146.1 1.7 %reshape.26 = f32[64,2,4,1024]{3,2,1,0:T(4,128)} reshape(bf16[64,8,1024]{2,1,0:T(8,128)(2,1)S(1)} %gather_fusion.1) | data formatting | bytes 3145728 | tf_op jit(solution)/shard_map/convert_element_type | solution.py:274
  (7 shorter events, 0.1 us)
Async XLA Ops:
  0.0 1.2 copy-start
  1.2 16.6 %copy-start.2 = (bf16[2,2,128,1024]{3,2,1,0:T(8,128)(2,1)S(1)}, bf16[2,2,128,1024]{3,2,1,0:T(8,128)(2,1)}, u32[]{:S(2)}) copy-start(bf16[2,2,128,1024]{3,2,1,0:T(8,128)(2,1)} %param.4) | copy-start | bytes 3145732
  2.9 75.9 %copy-start.3 = (s32[2,1024]{1,0:T(2,128)S(1)}, s32[2,1024]{1,0:T(2,128)}, u32[]{:S(2)}) copy-start(s32[2,1024]{1,0:T(2,128)} %param.7) | copy-start | bytes 24580
  2.9 78.4 %all-to-all-start = ((bf16[64,2,32,128]{3,2,1,0:T(8,128)(2,1)}), bf16[64,2,32,128]{3,2,1,0:T(8,128)(2,1)}, u32[]{:S(2)}, u32[]{:S(2)}) async-start(bf16[64,2,32,128]{3,2,1,0:T(8,128)(2,1)} %gather_fusion), calls=%async_computation | async-start | bytes 2097152 | tf_op jit(solution)/shard_map/all_to_all | solution.py:33
  17.9 47.1 %collective-permute-start.2 = (bf16[2,128,1024]{2,1,0:T(8,128)(2,1)S(1)}, bf16[2,128,1024]{2,1,0:T(8,128)(2,1)}, u32[]{:S(2)}, u32[]{:S(2)}) collective-permute-start(bf16[2,128,1024]{2,1,0:T(8,128)(2,1)S(1)} %dynamic-slice_bitcast_fusion.1), channel_id=1, source_target_pairs={{0,4},{4,0},{1,5},{5,1},{2,6},{6,2},{3,7},{7,3},{8,12},{12,8},{9,1... | collective-permute-start | bytes 1572872 | tf_op jit(solution)/shard_map/ppermute | solution.py:21
  21.2 43.8 %collective-permute-start = (bf16[2,128,1024]{2,1,0:T(8,128)(2,1)}, bf16[2,128,1024]{2,1,0:T(8,128)(2,1)}, u32[]{:S(2)}, u32[]{:S(2)}) collective-permute-start(bf16[2,128,1024]{2,1,0:T(8,128)(2,1)} %dynamic-slice_bitcast_fusion.refs_0_), channel_id=1, source_target_pairs={{0,2},{2,0},{1,3},{3,1},{4,6},{6,4},{5,7},{7,5},{8,10},{10,8},{9,1... | collective-permute-start | bytes 1572872 | tf_op jit(solution)/shard_map/ppermute | solution.py:21
  65.1 13.7 %collective-permute-start.5 = (bf16[2,128,1024]{2,1,0:T(8,128)(2,1)}, bf16[2,128,1024]{2,1,0:T(8,128)(2,1)}, u32[]{:S(2)}, u32[]{:S(2)}) collective-permute-start(bf16[2,128,1024]{2,1,0:T(8,128)(2,1)} %collective-permute-done.2.refs_1_), channel_id=1, source_target_pairs={{0,2},{2,0},{1,3},{3,1},{4,6},{6,4},{5,7},{7,5},{8,10},{10,8},{9,1... | collective-permute-start | bytes 1572872 | tf_op jit(solution)/shard_map/ppermute | solution.py:21
  65.1 16.2 %collective-permute-start.1 = (bf16[2,128,1024]{2,1,0:T(8,128)(2,1)}, bf16[2,128,1024]{2,1,0:T(8,128)(2,1)}, u32[]{:S(2)}, u32[]{:S(2)}) collective-permute-start(bf16[2,128,1024]{2,1,0:T(8,128)(2,1)} %collective-permute-done.refs_0_), channel_id=1, source_target_pairs={{0,1},{1,0},{2,3},{3,2},{4,5},{5,4},{6,7},{7,6},{8,9},{9,8},{10,11... | collective-permute-start | bytes 1572872 | tf_op jit(solution)/shard_map/ppermute | solution.py:21
  65.1 19.7 %collective-permute-start.3 = (bf16[2,128,1024]{2,1,0:T(8,128)(2,1)}, bf16[2,128,1024]{2,1,0:T(8,128)(2,1)}, u32[]{:S(2)}, u32[]{:S(2)}) collective-permute-start(bf16[2,128,1024]{2,1,0:T(8,128)(2,1)} %dynamic-slice_bitcast_fusion.refs_0_), channel_id=1, source_target_pairs={{0,1},{1,0},{2,3},{3,2},{4,5},{5,4},{6,7},{7,6},{8,9},{9,8},{10,11... | collective-permute-start | bytes 1572872 | tf_op jit(solution)/shard_map/ppermute | solution.py:21
  65.6 19.2 %collective-permute-start.4 = (bf16[2,128,1024]{2,1,0:T(8,128)(2,1)}, bf16[2,128,1024]{2,1,0:T(8,128)(2,1)}, u32[]{:S(2)}, u32[]{:S(2)}) collective-permute-start(bf16[2,128,1024]{2,1,0:T(8,128)(2,1)} %collective-permute-done.2.refs_1_), channel_id=1, source_target_pairs={{0,1},{1,0},{2,3},{3,2},{4,5},{5,4},{6,7},{7,6},{8,9},{9,8},{10,11... | collective-permute-start | bytes 1572872 | tf_op jit(solution)/shard_map/ppermute | solution.py:21
  78.8 9.8 %collective-permute-start.6 = (bf16[2,128,1024]{2,1,0:T(8,128)(2,1)}, bf16[2,128,1024]{2,1,0:T(8,128)(2,1)}, u32[]{:S(2)}, u32[]{:S(2)}) collective-permute-start(bf16[2,128,1024]{2,1,0:T(8,128)(2,1)} %collective-permute-done.5.w_ref), channel_id=1, source_target_pairs={{0,1},{1,0},{2,3},{3,2},{4,5},{5,4},{6,7},{7,6},{8,9},{9,8},{10,11... | collective-permute-start | bytes 1572872 | tf_op jit(solution)/shard_map/ppermute | solution.py:21
  79.8 1.0 copy-start.1
  87.6 14.3 %collective-permute-start.7 = (bf16[2,2,128,256]{3,2,1,0:T(8,128)(2,1)S(1)}, bf16[2,2,128,256]{3,2,1,0:T(8,128)(2,1)S(1)}, u32[]{:S(2)}, u32[]{:S(2)}) collective-permute-start(bf16[2,2,128,256]{3,2,1,0:T(8,128)(2,1)S(1)} %get-tuple-element.22), channel_id=1, source_target_pairs={{0,1},{1,0},{2,3},{3,2},{4,5},{5,4},{6,7},{7,6},{8,9},{9,8},{10,11... | collective-permute-start | bytes 786440 | tf_op jit(solution)/shard_map/ppermute | solution.py:21
  88.2 6.9 %collective-permute-start.8 = (bf16[2,128,256]{2,1,0:T(8,128)(2,1)S(1)}, bf16[2,128,256]{2,1,0:T(8,128)(2,1)S(1)}, u32[]{:S(2)}, u32[]{:S(2)}) collective-permute-start(bf16[2,128,256]{2,1,0:T(8,128)(2,1)S(1)} %get-tuple-element.23), channel_id=1, source_target_pairs={{0,2},{2,0},{1,3},{3,1},{4,6},{6,4},{5,7},{7,5},{8,10},{10,8},{9,1... | collective-permute-start | bytes 393224 | tf_op jit(solution)/shard_map/ppermute | solution.py:21
  91.5 5.8 %collective-permute-start.9 = (bf16[2,128,256]{2,1,0:T(8,128)(2,1)S(1)}, bf16[2,128,256]{2,1,0:T(8,128)(2,1)S(1)}, u32[]{:S(2)}, u32[]{:S(2)}) collective-permute-start(bf16[2,128,256]{2,1,0:T(8,128)(2,1)S(1)} %get-tuple-element.24), channel_id=1, source_target_pairs={{0,2},{2,0},{1,3},{3,1},{4,6},{6,4},{5,7},{7,5},{8,10},{10,8},{9,1... | collective-permute-start | bytes 393224 | tf_op jit(solution)/shard_map/ppermute | solution.py:21
  93.4 6.7 %collective-permute-start.10 = (bf16[2,128,256]{2,1,0:T(8,128)(2,1)S(1)}, bf16[2,128,256]{2,1,0:T(8,128)(2,1)S(1)}, u32[]{:S(2)}, u32[]{:S(2)}) collective-permute-start(bf16[2,128,256]{2,1,0:T(8,128)(2,1)S(1)} %get-tuple-element.25), channel_id=1, source_target_pairs={{0,3},{1,2},{2,1},{3,0},{4,7},{5,6},{6,5},{7,4},{8,11},{9,10},{10,... | collective-permute-start | bytes 393224 | tf_op jit(solution)/shard_map/ppermute | solution.py:21
  93.4 8.6 %collective-permute-start.11 = (bf16[2,128,256]{2,1,0:T(8,128)(2,1)S(1)}, bf16[2,128,256]{2,1,0:T(8,128)(2,1)S(1)}, u32[]{:S(2)}, u32[]{:S(2)}) collective-permute-start(bf16[2,128,256]{2,1,0:T(8,128)(2,1)S(1)} %get-tuple-element.26), channel_id=1, source_target_pairs={{0,3},{1,2},{2,1},{3,0},{4,7},{5,6},{6,5},{7,4},{8,11},{9,10},{10,... | collective-permute-start | bytes 393224 | tf_op jit(solution)/shard_map/ppermute | solution.py:21
  105.4 11.4 %copy-start.4 = (s32[64]{0:T(128)S(1)}, s32[64]{0:T(128)}, u32[]{:S(2)}) copy-start(s32[64]{0:T(128)} %param.6) | copy-start | bytes 772
  105.4 40.1 %all-to-all-start.1 = ((bf16[64,8,1024]{2,1,0:T(8,128)(2,1)}), bf16[64,8,1024]{2,1,0:T(8,128)(2,1)S(1)}, u32[]{:S(2)}, u32[]{:S(2)}) async-start(bf16[64,8,1024]{2,1,0:T(8,128)(2,1)} %bitcast.7), calls=%async_computation.1 | async-start | bytes 2097152 | tf_op jit(solution)/shard_map/all_to_all | solution.py:33

commit v5 on v4

--- a/solution.py
+++ b/solution.py
@@ -230,6 +230,28 @@
     )(side, *near([*weights, *halves]))
 
 
+def order_back_kernel(owner_ref, found_ref, out_ref):
+    count = out_ref.shape[0]
+    base = pl.program_id(0) * count
+    for j in range(count):
+        value = found_ref[owner_ref[base + j]].astype(jnp.float32)
+        out_ref[j, 0] = value[:4]
+        out_ref[j, 1] = value[4:]
+
+
+def order_back(q_owner, found):
+    slots, _, size = found.shape
+    return pl.pallas_call(
+        order_back_kernel,
+        grid=(4,),
+        out_shape=jax.ShapeDtypeStruct((slots, 2, 4, size), jnp.float32),
+        in_specs=[pl.BlockSpec(memory_space=pltpu.SMEM), DENSE],
+        out_specs=pl.BlockSpec((slots // 4, 2, 4, size), lambda i: (i, 0, 0, 0)),
+        compiler_params=PARAMS,
+        name="order_back",
+    )(q_owner, *near([found]))
+
+
 def steps(screened, response, q_owner, g_index):
     slots = q_owner.shape[0]
     _, parts, _, size = screened.shape
@@ -270,8 +292,7 @@
 
     result = tangent_product(side, (four, first_two, last_two), halves)
     returned = spread(result.reshape(slots, parts * 4, size))
-    returned = returned.at[q_owner].get(mode="promise_in_bounds")
-    return returned.reshape(slots, parts, 4, size).astype(jnp.float32)
+    return order_back(q_owner, returned)
 
 
 def solution(mesh):

time: 150 us -> 149 us (level)
  blocking collectives: 0 us -> 39.9 us
  waiting for transfers between devices: 91.4 us -> 62.8 us
  starting transfers between devices: 34.9 us -> 23.5 us
  local copies, waits for them, and re-layouts: 7.29 us -> 5.04 us
    all_to_all x0 -> x1, blocking collectives: none -> 39.9 us  [spread(): return lax.all_to_all(x, SPREAD, 0, 0, tiled=True)]
    all_to_all x2 -> x1, waiting for transfers between devices: 28.6 us -> 0.01 us  [spread(): return lax.all_to_all(x, SPREAD, 0, 0, tiled=True)]
    all_to_all x2 -> x1, starting transfers between devices: 26.4 us -> 15 us  [spread(): return lax.all_to_all(x, SPREAD, 0, 0, tiled=True)]
    pallas_call x0 -> x1, Pallas kernels: none -> 2.39 us  [order_back(): pl.pallas_call(order_back_kernel, grid=(4,), out_shape=jax.ShapeDtypeStru...]
    convert_element_type x1 -> x0, local copies, waits for them, and re-layouts: 1.67 us -> none  [steps(): return returned.reshape(slots, parts, 4, size).astype(jnp.float32)]
  transfers between devices with their start and end apart: 14 -> 13, of which waited for: 6 -> 5; matrix products, arithmetic and copies ran while one was open for 1% -> 1% of each run, Pallas kernels for 7% -> 7%
where the time goes in v5:
time: 149 us; the launch traced here: 147 us
  waiting for transfers between devices  62.8 us (42%)
  blocking collectives  39.9 us (27%)
  starting transfers between devices  23.5 us (16%)
  Pallas kernels  14.6 us (10%)
  local copies, waits for them, and re-layouts  5.04 us (3%)
    ppermute x12, waiting for transfers between devices, swap(): return lax.ppermute(x, axes, [(i, i ^ mask) for i in range(count)])  62.7 us
    all_to_all x1, blocking collectives, spread(): return lax.all_to_all(x, SPREAD, 0, 0, tiled=True)  39.9 us
    all_to_all x1, starting transfers between devices, spread(): return lax.all_to_all(x, SPREAD, 0, 0, tiled=True)  15 us
    ppermute x12, starting transfers between devices, swap(): return lax.ppermute(x, axes, [(i, i ^ mask) for i in range(count)])  8.51 us
    pallas_call x1, Pallas kernels, early_half(): pl.pallas_call(early_kernel, out_shape=[VMEM((size, 4 * width), jnp.bfloa...  3.41 us
    pallas_call x1, Pallas kernels, pair_half(): pl.pallas_call(pair_kernel, out_shape=[one, one, VMEM((2, 2, rows, size),...  3 us
  transfers between devices with their start and end apart: 13, of which 5 were waited for; matrix products, arithmetic and copies ran while one was open for 1% of the time, Pallas kernels for 7%

profile of v5, /device:TPU:2, one launch (start us, length us, event | category | flops | bytes accessed | tf_op | source)
XLA Modules:
  0.0 146.8 jit_solution(792023110474132349)
XLA Ops:
  0.0 0.0 copy-start
  0.0 0.8 select_reduce_fusion
  0.9 0.4 copy-done
  1.2 0.0 copy-start.3
  1.2 1.6 %gather_fusion = bf16[64,2,32,128]{3,2,1,0:T(8,128)(2,1)} fusion(bf16[64,2,32,128]{3,2,1,0:T(8,128)(2,1)S(1)} %copy-done, s32[1024]{0:T(1024)S(1)} %pad_clamp_fusion), kind=kCustom, calls=%fused_computation | custom fusion | bytes 2097408 | tf_op jit(solution)/shard_map/gather | solution.py:274
  2.9 0.0 copy-start.4
  2.9 15.0 %all-to-all-start = ((bf16[64,2,32,128]{3,2,1,0:T(8,128)(2,1)}), bf16[64,2,32,128]{3,2,1,0:T(8,128)(2,1)}, u32[]{:S(2)}, u32[]{:S(2)}) async-start(bf16[64,2,32,128]{3,2,1,0:T(8,128)(2,1)} %gather_fusion), calls=%async_computation | async-start | bytes 2097152 | tf_op jit(solution)/shard_map/all_to_all | solution.py:33
  17.9 0.0 copy-done.3
  17.9 2.4 %collective-permute-start.2 = (bf16[2,128,1024]{2,1,0:T(8,128)(2,1)S(1)}, bf16[2,128,1024]{2,1,0:T(8,128)(2,1)}, u32[]{:S(2)}, u32[]{:S(2)}) collective-permute-start(bf16[2,128,1024]{2,1,0:T(8,128)(2,1)S(1)} %dynamic-slice_bitcast_fusion.1), channel_id=1, source_target_pairs={{0,4},{4,0},{1,5},{5,1},{2,6},{6,2},{3,7},{7,3},{8,12},{12,8},{9,1... | collective-permute-start | bytes 1572872 | tf_op jit(solution)/shard_map/ppermute | solution.py:21
  20.4 0.9 dynamic-slice_bitcast_fusion.refs_0_
  21.2 1.0 collective-permute-start
  22.3 42.8 %collective-permute-done.2.refs_1_ = bf16[2,128,1024]{2,1,0:T(8,128)(2,1)} collective-permute-done((bf16[2,128,1024]{2,1,0:T(8,128)(2,1)S(1)}, bf16[2,128,1024]{2,1,0:T(8,128)(2,1)}, u32[]{:S(2)}, u32[]{:S(2)}) %collective-permute-start.2) | collective-permute-done | bytes 524320 | tf_op jit(solution)/shard_map/ppermute | solution.py:21
  65.1 0.0 collective-permute-start.5
  65.1 0.0 collective-permute-done.refs_0_
  65.1 0.0 collective-permute-start.1
  65.1 0.5 collective-permute-start.3
  65.6 0.1 collective-permute-start.4
  65.7 13.1 %collective-permute-done.5.w_ref = bf16[2,128,1024]{2,1,0:T(8,128)(2,1)} collective-permute-done((bf16[2,128,1024]{2,1,0:T(8,128)(2,1)}, bf16[2,128,1024]{2,1,0:T(8,128)(2,1)}, u32[]{:S(2)}, u32[]{:S(2)}) %collective-permute-start.5) | collective-permute-done | bytes 524320 | tf_op jit(solution)/shard_map/ppermute | solution.py:21
  78.8 0.0 collective-permute-start.6
  78.8 0.0 copy-done.4
  78.8 1.1 copy.6.table_ref
  79.8 0.0 copy-start.1
  79.8 1.0 copy-done.1
  80.9 0.4 order.1.order_ref
  81.3 0.0 collective-permute-done.1.refs_1_
  81.3 0.0 all-to-all-done
  81.3 3.4 %early.1 = (bf16[1024,512]{1,0:T(8,128)(2,1)S(1)}, bf16[2,128,256]{2,1,0:T(8,128)(2,1)S(1)}, bf16[2,128,256]{2,1,0:T(8,128)(2,1)S(1)}, bf16[2,2,128,1024]{3,2,1,0:T(8,128)(2,1)S(1)}) custom-call(s32[1]{0:T(128)} %bitcast.side_ref, bf16[1024,1024]{1,0:T(8,128)(2,1)S(1)} %order.1.order_ref, bf16[32,2,2,32,128]{4,3,2,1,0:T(8,128)(2,1)} %bitcast.4.landed_ref, ...), custom_call_target="tpu_custom_call" | custom-call | flops 1610612736 | bytes 5242880 | tf_op jit(solution)/shard_map/early/pallas_call | solution.py:103
  84.7 0.0 collective-permute-done.3.refs_2_
  84.8 0.0 collective-permute-done.4.refs_3_
  84.8 2.9 %inside.1 = (bf16[2,2,128,256]{3,2,1,0:T(8,128)(2,1)S(1)}, bf16[2,2,128,256]{3,2,1,0:T(8,128)(2,1)S(1)}, bf16[2,4,128,1024]{3,2,1,0:T(8,128)(2,1)S(1)}) custom-call(bf16[1024,512]{1,0:T(8,128)(2,1)S(1)} %get-tuple-element.17.both_ref, bf16[2,128,1024]{2,1,0:T(8,128)(2,1)} %dynamic-slice_bitcast_fusion.refs_0_, ...), custom_call_target="tpu_custom_call" | custom-call | flops 1073741824 | bytes 4194304 | tf_op jit(solution)/shard_map/inside/pallas_call | solution.py:164
  87.7 0.6 collective-permute-start.7
  88.3 0.3 collective-permute-start.8
  88.6 0.0 collective-permute-done.6.v_ref
  88.6 3.0 %shard_map.46 = (bf16[2,128,256]{2,1,0:T(8,128)(2,1)S(1)}, bf16[2,128,256]{2,1,0:T(8,128)(2,1)S(1)}, bf16[2,2,128,1024]{3,2,1,0:T(8,128)(2,1)S(1)}) custom-call(bf16[1024,512]{1,0:T(8,128)(2,1)S(1)} %get-tuple-element.17.both_ref, bf16[2,128,1024]{2,1,0:T(8,128)(2,1)} %collective-permute-done.5.w_ref, bf16[2,128,1024]{2,1,0:T(8,128)(2,1)} %collective-permute-done.6.v_ref), custom_call_target="tpu_custom_call" | custom-call | flops 536870912 | bytes 2097152 | tf_op jit(solution)/shard_map/pallas_call | solution.py:136
  91.6 1.8 %collective-permute-start.9 = (bf16[2,128,256]{2,1,0:T(8,128)(2,1)S(1)}, bf16[2,128,256]{2,1,0:T(8,128)(2,1)S(1)}, u32[]{:S(2)}, u32[]{:S(2)}) collective-permute-start(bf16[2,128,256]{2,1,0:T(8,128)(2,1)S(1)} %get-tuple-element.24), channel_id=1, source_target_pairs={{0,2},{2,0},{1,3},{3,1},{4,6},{6,4},{5,7},{7,5},{8,10},{10,8},{9,1... | collective-permute-start | bytes 393224 | tf_op jit(solution)/shard_map/ppermute | solution.py:21
  93.4 0.0 collective-permute-start.10
  93.4 1.7 %collective-permute-start.11 = (bf16[2,128,256]{2,1,0:T(8,128)(2,1)S(1)}, bf16[2,128,256]{2,1,0:T(8,128)(2,1)S(1)}, u32[]{:S(2)}, u32[]{:S(2)}) collective-permute-start(bf16[2,128,256]{2,1,0:T(8,128)(2,1)S(1)} %get-tuple-element.26), channel_id=1, source_target_pairs={{0,3},{1,2},{2,1},{3,0},{4,7},{5,6},{6,5},{7,4},{8,11},{9,10},{10,... | collective-permute-start | bytes 393224 | tf_op jit(solution)/shard_map/ppermute | solution.py:21
  95.1 0.0 collective-permute-done.8.refs_2_
  95.1 2.3 %collective-permute-done.9.refs_3_ = bf16[2,128,256]{2,1,0:T(8,128)(2,1)S(1)} collective-permute-done((bf16[2,128,256]{2,1,0:T(8,128)(2,1)S(1)}, bf16[2,128,256]{2,1,0:T(8,128)(2,1)S(1)}, u32[]{:S(2)}, u32[]{:S(2)}) %collective-permute-start.9) | collective-permute-done | bytes 131104 | tf_op jit(solution)/shard_map/ppermute | solution.py:21
  97.4 2.7 %collective-permute-done.10.refs_4_ = bf16[2,128,256]{2,1,0:T(8,128)(2,1)S(1)} collective-permute-done((bf16[2,128,256]{2,1,0:T(8,128)(2,1)S(1)}, bf16[2,128,256]{2,1,0:T(8,128)(2,1)S(1)}, u32[]{:S(2)}, u32[]{:S(2)}) %collective-permute-start.10) | collective-permute-done | bytes 131104 | tf_op jit(solution)/shard_map/ppermute | solution.py:21
  100.1 1.9 %collective-permute-done.11.refs_5_ = bf16[2,128,256]{2,1,0:T(8,128)(2,1)S(1)} collective-permute-done((bf16[2,128,256]{2,1,0:T(8,128)(2,1)S(1)}, bf16[2,128,256]{2,1,0:T(8,128)(2,1)S(1)}, u32[]{:S(2)}, u32[]{:S(2)}) %collective-permute-start.11) | collective-permute-done | bytes 131104 | tf_op jit(solution)/shard_map/ppermute | solution.py:21
  102.0 0.0 collective-permute-done.7.refs_1_
  102.0 2.5 %tangent.1 = bf16[32,2,8,1024]{3,2,1,0:T(8,128)(2,1)S(1)} custom-call(s32[1]{0:T(128)} %bitcast.side_ref, bf16[2,4,128,1024]{3,2,1,0:T(8,128)(2,1)S(1)} %get-tuple-element.18.four, bf16[2,2,128,1024]{3,2,1,0:T(8,128)(2,1)S(1)} %get-tuple-element.19.first_two, bf16[2,2,128,1024]{3,2,1,0:T(8,128)(2,1)S(1)} %get-tuple-element.20.last_two, ...), custom_call_target="tpu_custom_call" | custom-call | flops 2147483648 | bytes 3145728 | tf_op jit(solution)/shard_map/tangent/pallas_call | solution.py:219
  104.5 0.0 copy-start.2
  104.5 39.9 %all_to_all.10.found_ref = bf16[64,8,1024]{2,1,0:T(8,128)(2,1)S(1)} all-to-all(bf16[64,8,1024]{2,1,0:T(8,128)(2,1)S(1)} %bitcast.13), channel_id=1, replica_groups=mesh['zh'=2,'y'=4,'x'=4,'zm'=2,'zn'=2,'c'=2] {'zh','y','x','zm'}, dimensions={0} | all-to-all | bytes 2097152 | tf_op jit(solution)/shard_map/all_to_all | solution.py:33
  144.4 0.0 copy-done.2
  144.4 2.4 %order_back.1 = f32[64,2,4,1024]{3,2,1,0:T(4,128)} custom-call(s32[64]{0:T(128)S(1)} %copy-done.2, bf16[64,8,1024]{2,1,0:T(8,128)(2,1)S(1)} %all_to_all.10.found_ref), custom_call_target="tpu_custom_call" | custom-call | tf_op jit(solution)/shard_map/order_back/pallas_call | solution.py:244
  (4 shorter events, 0.1 us)
Async XLA Ops:
  0.0 1.2 copy-start
  1.2 16.6 %copy-start.3 = (bf16[2,2,128,1024]{3,2,1,0:T(8,128)(2,1)S(1)}, bf16[2,2,128,1024]{3,2,1,0:T(8,128)(2,1)}, u32[]{:S(2)}) copy-start(bf16[2,2,128,1024]{3,2,1,0:T(8,128)(2,1)} %param.4) | copy-start | bytes 3145732
  2.9 75.9 %copy-start.4 = (s32[2,1024]{1,0:T(2,128)S(1)}, s32[2,1024]{1,0:T(2,128)}, u32[]{:S(2)}) copy-start(s32[2,1024]{1,0:T(2,128)} %param.7) | copy-start | bytes 24580
  2.9 78.4 %all-to-all-start = ((bf16[64,2,32,128]{3,2,1,0:T(8,128)(2,1)}), bf16[64,2,32,128]{3,2,1,0:T(8,128)(2,1)}, u32[]{:S(2)}, u32[]{:S(2)}) async-start(bf16[64,2,32,128]{3,2,1,0:T(8,128)(2,1)} %gather_fusion), calls=%async_computation | async-start | bytes 2097152 | tf_op jit(solution)/shard_map/all_to_all | solution.py:33
  17.9 47.1 %collective-permute-start.2 = (bf16[2,128,1024]{2,1,0:T(8,128)(2,1)S(1)}, bf16[2,128,1024]{2,1,0:T(8,128)(2,1)}, u32[]{:S(2)}, u32[]{:S(2)}) collective-permute-start(bf16[2,128,1024]{2,1,0:T(8,128)(2,1)S(1)} %dynamic-slice_bitcast_fusion.1), channel_id=1, source_target_pairs={{0,4},{4,0},{1,5},{5,1},{2,6},{6,2},{3,7},{7,3},{8,12},{12,8},{9,1... | collective-permute-start | bytes 1572872 | tf_op jit(solution)/shard_map/ppermute | solution.py:21
  21.2 43.8 %collective-permute-start = (bf16[2,128,1024]{2,1,0:T(8,128)(2,1)}, bf16[2,128,1024]{2,1,0:T(8,128)(2,1)}, u32[]{:S(2)}, u32[]{:S(2)}) collective-permute-start(bf16[2,128,1024]{2,1,0:T(8,128)(2,1)} %dynamic-slice_bitcast_fusion.refs_0_), channel_id=1, source_target_pairs={{0,2},{2,0},{1,3},{3,1},{4,6},{6,4},{5,7},{7,5},{8,10},{10,8},{9,1... | collective-permute-start | bytes 1572872 | tf_op jit(solution)/shard_map/ppermute | solution.py:21
  65.1 13.7 %collective-permute-start.5 = (bf16[2,128,1024]{2,1,0:T(8,128)(2,1)}, bf16[2,128,1024]{2,1,0:T(8,128)(2,1)}, u32[]{:S(2)}, u32[]{:S(2)}) collective-permute-start(bf16[2,128,1024]{2,1,0:T(8,128)(2,1)} %collective-permute-done.2.refs_1_), channel_id=1, source_target_pairs={{0,2},{2,0},{1,3},{3,1},{4,6},{6,4},{5,7},{7,5},{8,10},{10,8},{9,1... | collective-permute-start | bytes 1572872 | tf_op jit(solution)/shard_map/ppermute | solution.py:21
  65.1 16.2 %collective-permute-start.1 = (bf16[2,128,1024]{2,1,0:T(8,128)(2,1)}, bf16[2,128,1024]{2,1,0:T(8,128)(2,1)}, u32[]{:S(2)}, u32[]{:S(2)}) collective-permute-start(bf16[2,128,1024]{2,1,0:T(8,128)(2,1)} %collective-permute-done.refs_0_), channel_id=1, source_target_pairs={{0,1},{1,0},{2,3},{3,2},{4,5},{5,4},{6,7},{7,6},{8,9},{9,8},{10,11... | collective-permute-start | bytes 1572872 | tf_op jit(solution)/shard_map/ppermute | solution.py:21
  65.1 19.7 %collective-permute-start.3 = (bf16[2,128,1024]{2,1,0:T(8,128)(2,1)}, bf16[2,128,1024]{2,1,0:T(8,128)(2,1)}, u32[]{:S(2)}, u32[]{:S(2)}) collective-permute-start(bf16[2,128,1024]{2,1,0:T(8,128)(2,1)} %dynamic-slice_bitcast_fusion.refs_0_), channel_id=1, source_target_pairs={{0,1},{1,0},{2,3},{3,2},{4,5},{5,4},{6,7},{7,6},{8,9},{9,8},{10,11... | collective-permute-start | bytes 1572872 | tf_op jit(solution)/shard_map/ppermute | solution.py:21
  65.6 19.2 %collective-permute-start.4 = (bf16[2,128,1024]{2,1,0:T(8,128)(2,1)}, bf16[2,128,1024]{2,1,0:T(8,128)(2,1)}, u32[]{:S(2)}, u32[]{:S(2)}) collective-permute-start(bf16[2,128,1024]{2,1,0:T(8,128)(2,1)} %collective-permute-done.2.refs_1_), channel_id=1, source_target_pairs={{0,1},{1,0},{2,3},{3,2},{4,5},{5,4},{6,7},{7,6},{8,9},{9,8},{10,11... | collective-permute-start | bytes 1572872 | tf_op jit(solution)/shard_map/ppermute | solution.py:21
  78.8 9.8 %collective-permute-start.6 = (bf16[2,128,1024]{2,1,0:T(8,128)(2,1)}, bf16[2,128,1024]{2,1,0:T(8,128)(2,1)}, u32[]{:S(2)}, u32[]{:S(2)}) collective-permute-start(bf16[2,128,1024]{2,1,0:T(8,128)(2,1)} %collective-permute-done.5.w_ref), channel_id=1, source_target_pairs={{0,1},{1,0},{2,3},{3,2},{4,5},{5,4},{6,7},{7,6},{8,9},{9,8},{10,11... | collective-permute-start | bytes 1572872 | tf_op jit(solution)/shard_map/ppermute | solution.py:21
  79.8 1.0 copy-start.1
  87.7 14.3 %collective-permute-start.7 = (bf16[2,2,128,256]{3,2,1,0:T(8,128)(2,1)S(1)}, bf16[2,2,128,256]{3,2,1,0:T(8,128)(2,1)S(1)}, u32[]{:S(2)}, u32[]{:S(2)}) collective-permute-start(bf16[2,2,128,256]{3,2,1,0:T(8,128)(2,1)S(1)} %get-tuple-element.22), channel_id=1, source_target_pairs={{0,1},{1,0},{2,3},{3,2},{4,5},{5,4},{6,7},{7,6},{8,9},{9,8},{10,11... | collective-permute-start | bytes 786440 | tf_op jit(solution)/shard_map/ppermute | solution.py:21
  88.3 6.9 %collective-permute-start.8 = (bf16[2,128,256]{2,1,0:T(8,128)(2,1)S(1)}, bf16[2,128,256]{2,1,0:T(8,128)(2,1)S(1)}, u32[]{:S(2)}, u32[]{:S(2)}) collective-permute-start(bf16[2,128,256]{2,1,0:T(8,128)(2,1)S(1)} %get-tuple-element.23), channel_id=1, source_target_pairs={{0,2},{2,0},{1,3},{3,1},{4,6},{6,4},{5,7},{7,5},{8,10},{10,8},{9,1... | collective-permute-start | bytes 393224 | tf_op jit(solution)/shard_map/ppermute | solution.py:21
  91.6 5.8 %collective-permute-start.9 = (bf16[2,128,256]{2,1,0:T(8,128)(2,1)S(1)}, bf16[2,128,256]{2,1,0:T(8,128)(2,1)S(1)}, u32[]{:S(2)}, u32[]{:S(2)}) collective-permute-start(bf16[2,128,256]{2,1,0:T(8,128)(2,1)S(1)} %get-tuple-element.24), channel_id=1, source_target_pairs={{0,2},{2,0},{1,3},{3,1},{4,6},{6,4},{5,7},{7,5},{8,10},{10,8},{9,1... | collective-permute-start | bytes 393224 | tf_op jit(solution)/shard_map/ppermute | solution.py:21
  93.4 6.7 %collective-permute-start.10 = (bf16[2,128,256]{2,1,0:T(8,128)(2,1)S(1)}, bf16[2,128,256]{2,1,0:T(8,128)(2,1)S(1)}, u32[]{:S(2)}, u32[]{:S(2)}) collective-permute-start(bf16[2,128,256]{2,1,0:T(8,128)(2,1)S(1)} %get-tuple-element.25), channel_id=1, source_target_pairs={{0,3},{1,2},{2,1},{3,0},{4,7},{5,6},{6,5},{7,4},{8,11},{9,10},{10,... | collective-permute-start | bytes 393224 | tf_op jit(solution)/shard_map/ppermute | solution.py:21
  93.4 8.6 %collective-permute-start.11 = (bf16[2,128,256]{2,1,0:T(8,128)(2,1)S(1)}, bf16[2,128,256]{2,1,0:T(8,128)(2,1)S(1)}, u32[]{:S(2)}, u32[]{:S(2)}) collective-permute-start(bf16[2,128,256]{2,1,0:T(8,128)(2,1)S(1)} %get-tuple-element.26), channel_id=1, source_target_pairs={{0,3},{1,2},{2,1},{3,0},{4,7},{5,6},{6,5},{7,4},{8,11},{9,10},{10,... | collective-permute-start | bytes 393224 | tf_op jit(solution)/shard_map/ppermute | solution.py:21
  104.5 39.9 %copy-start.2 = (s32[64]{0:T(128)S(1)}, s32[64]{0:T(128)}, u32[]{:S(2)}) copy-start(s32[64]{0:T(128)} %owner_ref.1) | copy-start | bytes 772
